TPU v7x, 32 devices: a whole 2x2x4 slice. The times are simulated.
32 devices in a mesh: gx: 4 (over x, core), gy: 8 (over z, y).
Axes of the slice: x: 2, y: 2, z: 4, core: 2. Of those that a mesh axis runs over, the one named last changes fastest.
Arguments:
- electric: float32 [3, 64, 128, 256], P(None, 'gx', 'gy'), may hold values from -6 to 6
- magnetic: float32 [3, 64, 128, 256], P(None, 'gx', 'gy'), may hold values from -6 to 6
- aux_electric: float32 [6, 64, 128, 256], P(None, 'gx', 'gy'), may hold values from -3 to 3
- aux_magnetic: float32 [6, 64, 128, 256], P(None, 'gx', 'gy'), may hold values from -3 to 3
- grades: int32 [3, 64, 128, 256], P(None, 'gx', 'gy'), may hold values from 0 to 3
- permittivity: float32 [64, 128, 256], P('gx', 'gy'), may hold values from 1 to 8
- dipole_cell: int32 [3, 16384], P(None, ('gx', 'gy')), may hold values from 0 to 255, as said below
- dipole_port: int32 [16384], P(('gx', 'gy')), may hold values from 0 to 511
- live_count: int32 [32], P(('gx', 'gy')), may hold values from 1 to 512, as said below
- injection: bfloat16 [16384, 512], P(('gx', 'gy')), may hold values from -0.25 to 0.25
- waveform: bfloat16 [512, 16], replicated, may hold values from -6 to 6
Outputs:
- electric_out: float32 [3, 64, 128, 256], P(None, 'gx', 'gy')
- magnetic_out: float32 [3, 64, 128, 256], P(None, 'gx', 'gy')
- port_power: float32 [16, 512], replicated
Inputs may be any that keep to these rules, and one draw needn't show every extreme that they name: `dipole_cell`: slot s lies in the block of cells held by the device that holds slot s. The live slots of a device are its first live_count ones; some device has all 512 live.
All inputs are finite; a program needn't handle non-finite values.
Results may differ from a plain program's by a relative error of at most 0.0003.
Values sent between devices are 32-bit elements; how exact they have to be, the bound alone decides.
No kernel may reach another device: no remote copies, remote signals or barrier semaphores. Data moves between devices by JAX's collectives and lax.ppermute only.
A program may use at most 128 MiB of HBM per device.

v0:
```python
import jax
import jax.numpy as jnp
from jax import lax
from jax.sharding import PartitionSpec as P

courant = 0.55
absorb_keep = (0.0, 0.92, 0.75, 0.45)
absorb_take = (0.0, -0.06, -0.18, -0.35)
derivative_pairs = ((2, 1), (1, 2), (0, 2), (2, 0), (1, 0), (0, 1))


def passed_along(block, axis, distance):
    devices = range(lax.axis_size(axis))
    route = [(i - distance, i) for i in devices if i - distance in devices]
    return lax.ppermute(block, axis, route)


def difference(values, axis, plane, forward):
    length = values.shape[axis]
    if plane is None:
        shape = list(values.shape)
        shape[axis] = 1
        plane = jnp.zeros(shape, values.dtype)
    if forward:
        after = jnp.concatenate([lax.slice_in_dim(values, 1, length, axis=axis), plane], axis)
        return after - values
    before = jnp.concatenate([plane, lax.slice_in_dim(values, 0, length - 1, axis=axis)], axis)
    return values - before


def grade_table(grades, table):
    result = jnp.zeros(grades.shape, jnp.float32)
    for level in range(1, 4):
        result = result + jnp.where(grades == level, table[level], 0.0)
    return result


def curl_parts(field, auxiliary, keep, take, planes, forward):
    terms = []
    updated = []
    for number, (component, axis) in enumerate(derivative_pairs):
        plane = None
        if planes is not None and axis == 0:
            plane = planes[0][component - 1]
        if planes is not None and axis == 1:
            plane = planes[1][component // 2]
        slope = difference(field[component], axis, plane, forward)
        carried = keep[axis] * auxiliary[number] + take[axis] * slope
        terms.append(slope + carried)
        updated.append(carried)
    rotation = (terms[0] - terms[1], terms[2] - terms[3], terms[4] - terms[5])
    return (rotation, tuple(updated))


def inject(z_plane, current_now, cell_table, depth_table):
    weighted = cell_table * current_now[:, None]
    source = lax.dot_general(
        weighted, depth_table, (((0,), (0,)), ((), ())), precision=lax.Precision.HIGHEST
    )
    return z_plane - courant * source.reshape(z_plane.shape)


def read_cells(z_plane, cell_table, depth_table):
    rows = z_plane.reshape(cell_table.shape[1], depth_table.shape[1])
    picked = jnp.dot(cell_table, rows, precision=lax.Precision.HIGHEST)
    return jnp.sum(picked * depth_table, axis=1)


def note_power(record, drive, index):
    return lax.dynamic_update_slice_in_dim(record, drive[None, :], index, 0)


def local(
    electric,
    magnetic,
    aux_electric,
    aux_magnetic,
    grades,
    permittivity,
    dipole_cell,
    dipole_port,
    live_count,
    injection,
    waveform,
):
    depth_x, depth_y, depth_z = electric.shape[1:]
    slots = dipole_cell.shape[1]
    ports, steps = waveform.shape
    row_index = lax.axis_index("gx")
    col_index = lax.axis_index("gy")
    plane_cell = (dipole_cell[0] - row_index * depth_x) * depth_y + (
        dipole_cell[1] - col_index * depth_y
    )
    cell_table = (
        plane_cell[:, None] == jnp.arange(depth_x * depth_y, dtype=jnp.int32)[None, :]
    ).astype(jnp.float32)
    depth_table = (dipole_cell[2][:, None] == jnp.arange(depth_z, dtype=jnp.int32)[None, :]).astype(
        jnp.float32
    )
    live = (jnp.arange(slots, dtype=jnp.int32) < live_count[0]).astype(jnp.float32)
    current = jnp.dot(injection, waveform, preferred_element_type=jnp.float32) * live[:, None]
    members = (dipole_port[:, None] == jnp.arange(ports, dtype=jnp.int32)[None, :]).astype(
        jnp.float32
    )
    factor = courant / permittivity
    keep = grade_table(grades, absorb_keep)
    take = grade_table(grades, absorb_take)
    record = jnp.zeros((steps, slots), jnp.float32)

    def turn_parts(step, carry):
        field_e, field_h, memory_e, memory_h, record = carry
        next_x = passed_along(jnp.stack([field_e[1][0:1], field_e[2][0:1]]), "gx", -1)
        next_y = passed_along(jnp.stack([field_e[0][:, 0:1], field_e[2][:, 0:1]]), "gy", -1)
        rotation, memory_e = curl_parts(field_e, memory_e, keep, take, (next_x, next_y), True)
        field_h = tuple((field_h[number] - courant * rotation[number] for number in range(3)))
        prior_x = passed_along(jnp.stack([field_h[1][-1:], field_h[2][-1:]]), "gx", 1)
        prior_y = passed_along(jnp.stack([field_h[0][:, -1:], field_h[2][:, -1:]]), "gy", 1)
        rotation, memory_h = curl_parts(field_h, memory_h, keep, take, (prior_x, prior_y), False)
        current_now = lax.dynamic_slice_in_dim(current, step, 1, 1)[:, 0]
        z_plane = inject(field_e[2] + factor * rotation[2], current_now, cell_table, depth_table)
        field_e = (field_e[0] + factor * rotation[0], field_e[1] + factor * rotation[1], z_plane)
        drive = current_now * read_cells(z_plane, cell_table, depth_table)
        record = note_power(record, drive, step)
        return (field_e, field_h, memory_e, memory_h, record)

    start_state = (
        tuple((electric[number] for number in range(3))),
        tuple((magnetic[number] for number in range(3))),
        tuple((aux_electric[number] for number in range(6))),
        tuple((aux_magnetic[number] for number in range(6))),
        record,
    )
    parts_e, parts_h, parts_me, parts_mh, record = lax.fori_loop(0, steps, turn_parts, start_state)
    electric = jnp.stack(parts_e)
    magnetic = jnp.stack(parts_h)
    partial_value = jnp.dot(record, members, precision=lax.Precision.HIGHEST)
    port_power = lax.psum(partial_value, ("gx", "gy"))
    return (electric, magnetic, port_power)


def solution(mesh):
    in_specs = (
        P(None, "gx", "gy", None),
        P(None, "gx", "gy", None),
        P(None, "gx", "gy", None),
        P(None, "gx", "gy", None),
        P(None, "gx", "gy", None),
        P("gx", "gy", None),
        P(None, ("gx", "gy")),
        P(("gx", "gy")),
        P(("gx", "gy")),
        P(("gx", "gy"), None),
        P(),
    )
    out_specs = (P(None, "gx", "gy", None), P(None, "gx", "gy", None), P())
    return jax.shard_map(local, mesh=mesh, in_specs=in_specs, out_specs=out_specs, check_vma=False)
```

profile of v0, /device:TPU:0, one launch (start us, length us, event | category | flops | bytes accessed | tf_op | source)
XLA Modules:
  0.0 605.0 jit_solution(2541762445763992828)
XLA Ops:
  10.5 545.4 %while.50 = (s32[]{:T(128)}, f32[16,16,256]{2,1,0:T(8,128)S(1)}, f32[16,16,256]{2,1,0:T(8,128)S(1)}, f32[16,16,256]{2,1,0:T(8,128)S(1)}, f32[16,16,256]{2,1,0:T(...) while((s32[]{:T(128)}, f32[16,16,256]{2,1,0:T(8,128)S(1)}, ...), condition=%wide.region_2.3_spmd.clone, body=%wide.region_0.2_spmd.clone.sunk | while | flops 812285952 | bytes 56044672 | solution.py:133
  20.5 2.4 multiply_subtract_fusion.7
  23.5 5.5 collective-permute-start.2
  30.9 2.8 collective-permute-start.3
  52.6 2.4 multiply_subtract_fusion.7
  55.6 5.4 collective-permute-start.2
  63.0 3.8 collective-permute-start.3
  85.7 2.4 multiply_subtract_fusion.7
  88.7 5.2 collective-permute-start.2
  95.8 5.3 collective-permute-start.3
  120.0 2.4 multiply_subtract_fusion.7
  123.0 5.2 collective-permute-start.2
  130.1 5.3 collective-permute-start.3
  154.3 2.4 multiply_subtract_fusion.7
  157.3 5.2 collective-permute-start.2
  164.4 5.3 collective-permute-start.3
  188.6 2.4 multiply_subtract_fusion.7
  191.6 5.2 collective-permute-start.2
  198.7 5.3 collective-permute-start.3
  222.9 2.4 multiply_subtract_fusion.7
  225.9 5.2 collective-permute-start.2
  233.0 5.3 collective-permute-start.3
  257.2 2.4 multiply_subtract_fusion.7
  260.2 5.2 collective-permute-start.2
  267.3 5.3 collective-permute-start.3
  291.5 2.4 multiply_subtract_fusion.7
  294.5 5.2 collective-permute-start.2
  301.6 5.3 collective-permute-start.3
  325.8 2.4 multiply_subtract_fusion.7
  328.8 5.2 collective-permute-start.2
  335.9 5.3 collective-permute-start.3
  360.1 2.4 multiply_subtract_fusion.7
  363.1 5.2 collective-permute-start.2
  370.2 5.3 collective-permute-start.3
  394.4 2.4 multiply_subtract_fusion.7
  397.4 5.2 collective-permute-start.2
  404.5 5.3 collective-permute-start.3
  428.7 2.4 multiply_subtract_fusion.7
  431.7 5.2 collective-permute-start.2
  438.8 5.3 collective-permute-start.3
  463.0 2.4 multiply_subtract_fusion.7
  466.0 5.2 collective-permute-start.2
  473.1 5.3 collective-permute-start.3
  500.3 5.2 collective-permute-start.2
  507.4 5.3 collective-permute-start.3
  534.6 5.2 collective-permute-start.2
  541.7 5.3 collective-permute-start.3
  557.2 45.9 %psum.7 = f32[16,512]{1,0:T(8,128)} all-reduce(f32[16,512]{1,0:T(8,128)S(1)} %fusion.27), channel_id=1, replica_groups=mesh['gx'=4,'gy'=8] {'gx','gy'}, use_global_device_ids=true, to_apply=%region_3.4 | all-reduce | flops 8192 | bytes 65536 | tf_op jit(solution)/shard_map/psum | solution.py:137
  (1470 shorter events, 352.0 us)
Async XLA Ops:
  10.6 9.9 %collective-permute-start.1 = (f32[2,16,1,256]{3,2,1,0:T(1,128)S(1)}, f32[2,16,1,256]{3,2,1,0:T(1,128)S(1)}, u32[]{:S(2)}, u32[]{:S(2)}) collective-permute-start(f32[2,16,1,256]{3,2,1,0:T(1,128)S(1)} %pad_maximum_fusion.11), channel_id=1, source_target_pairs={{1,0},{2,1},{3,2},{4,3},{5,4},{6,5},{7,6},{9,8},{10,9},{11,10},{12... | collective-permute-start | bytes 98312 | tf_op jit(solution)/shard_map/while/body/eval_jaxpr/ppermute | solution.py:15
  11.9 8.5 %collective-permute-start = (f32[2,1,16,256]{3,2,1,0:T(8,128)S(1)}, f32[2,1,16,256]{3,2,1,0:T(8,128)S(1)}, u32[]{:S(2)}, u32[]{:S(2)}) collective-permute-start(f32[2,1,16,256]{3,2,1,0:T(8,128)S(1)} %pad_maximum_fusion.10), channel_id=1, source_target_pairs={{8,0},{16,8},{24,16},{9,1},{17,9},{25,17},{10,2},{18,10},{26,18},{... | collective-permute-start | bytes 98312 | tf_op jit(solution)/shard_map/while/body/eval_jaxpr/ppermute | solution.py:15
  23.5 10.2 %collective-permute-start.2 = (f32[2,16,1,256]{3,2,1,0:T(1,128)S(1)}, f32[2,16,1,256]{3,2,1,0:T(1,128)S(1)}, u32[]{:S(2)}, u32[]{:S(2)}) collective-permute-start(f32[2,16,1,256]{3,2,1,0:T(1,128)S(1)} %pad_maximum_fusion.12), channel_id=1, source_target_pairs={{0,1},{1,2},{2,3},{3,4},{4,5},{5,6},{6,7},{8,9},{9,10},{10,11},{11... | collective-permute-start | bytes 98312 | tf_op jit(solution)/shard_map/while/body/eval_jaxpr/ppermute | solution.py:15
  42.7 9.9 %collective-permute-start.1 = (f32[2,16,1,256]{3,2,1,0:T(1,128)S(1)}, f32[2,16,1,256]{3,2,1,0:T(1,128)S(1)}, u32[]{:S(2)}, u32[]{:S(2)}) collective-permute-start(f32[2,16,1,256]{3,2,1,0:T(1,128)S(1)} %pad_maximum_fusion.11), channel_id=1, source_target_pairs={{1,0},{2,1},{3,2},{4,3},{5,4},{6,5},{7,6},{9,8},{10,9},{11,10},{12... | collective-permute-start | bytes 98312 | tf_op jit(solution)/shard_map/while/body/eval_jaxpr/ppermute | solution.py:15
  44.0 8.5 %collective-permute-start = (f32[2,1,16,256]{3,2,1,0:T(8,128)S(1)}, f32[2,1,16,256]{3,2,1,0:T(8,128)S(1)}, u32[]{:S(2)}, u32[]{:S(2)}) collective-permute-start(f32[2,1,16,256]{3,2,1,0:T(8,128)S(1)} %pad_maximum_fusion.10), channel_id=1, source_target_pairs={{8,0},{16,8},{24,16},{9,1},{17,9},{25,17},{10,2},{18,10},{26,18},{... | collective-permute-start | bytes 98312 | tf_op jit(solution)/shard_map/while/body/eval_jaxpr/ppermute | solution.py:15
  55.6 11.2 %collective-permute-start.2 = (f32[2,16,1,256]{3,2,1,0:T(1,128)S(1)}, f32[2,16,1,256]{3,2,1,0:T(1,128)S(1)}, u32[]{:S(2)}, u32[]{:S(2)}) collective-permute-start(f32[2,16,1,256]{3,2,1,0:T(1,128)S(1)} %pad_maximum_fusion.12), channel_id=1, source_target_pairs={{0,1},{1,2},{2,3},{3,4},{4,5},{5,6},{6,7},{8,9},{9,10},{10,11},{11... | collective-permute-start | bytes 98312 | tf_op jit(solution)/shard_map/while/body/eval_jaxpr/ppermute | solution.py:15
  75.8 9.9 %collective-permute-start.1 = (f32[2,16,1,256]{3,2,1,0:T(1,128)S(1)}, f32[2,16,1,256]{3,2,1,0:T(1,128)S(1)}, u32[]{:S(2)}, u32[]{:S(2)}) collective-permute-start(f32[2,16,1,256]{3,2,1,0:T(1,128)S(1)} %pad_maximum_fusion.11), channel_id=1, source_target_pairs={{1,0},{2,1},{3,2},{4,3},{5,4},{6,5},{7,6},{9,8},{10,9},{11,10},{12... | collective-permute-start | bytes 98312 | tf_op jit(solution)/shard_map/while/body/eval_jaxpr/ppermute | solution.py:15
  77.1 8.5 %collective-permute-start = (f32[2,1,16,256]{3,2,1,0:T(8,128)S(1)}, f32[2,1,16,256]{3,2,1,0:T(8,128)S(1)}, u32[]{:S(2)}, u32[]{:S(2)}) collective-permute-start(f32[2,1,16,256]{3,2,1,0:T(8,128)S(1)} %pad_maximum_fusion.10), channel_id=1, source_target_pairs={{8,0},{16,8},{24,16},{9,1},{17,9},{25,17},{10,2},{18,10},{26,18},{... | collective-permute-start | bytes 98312 | tf_op jit(solution)/shard_map/while/body/eval_jaxpr/ppermute | solution.py:15
  88.7 12.4 %collective-permute-start.2 = (f32[2,16,1,256]{3,2,1,0:T(1,128)S(1)}, f32[2,16,1,256]{3,2,1,0:T(1,128)S(1)}, u32[]{:S(2)}, u32[]{:S(2)}) collective-permute-start(f32[2,16,1,256]{3,2,1,0:T(1,128)S(1)} %pad_maximum_fusion.12), channel_id=1, source_target_pairs={{0,1},{1,2},{2,3},{3,4},{4,5},{5,6},{6,7},{8,9},{9,10},{10,11},{11... | collective-permute-start | bytes 98312 | tf_op jit(solution)/shard_map/while/body/eval_jaxpr/ppermute | solution.py:15
  110.1 9.9 %collective-permute-start.1 = (f32[2,16,1,256]{3,2,1,0:T(1,128)S(1)}, f32[2,16,1,256]{3,2,1,0:T(1,128)S(1)}, u32[]{:S(2)}, u32[]{:S(2)}) collective-permute-start(f32[2,16,1,256]{3,2,1,0:T(1,128)S(1)} %pad_maximum_fusion.11), channel_id=1, source_target_pairs={{1,0},{2,1},{3,2},{4,3},{5,4},{6,5},{7,6},{9,8},{10,9},{11,10},{12... | collective-permute-start | bytes 98312 | tf_op jit(solution)/shard_map/while/body/eval_jaxpr/ppermute | solution.py:15
  111.4 8.5 %collective-permute-start = (f32[2,1,16,256]{3,2,1,0:T(8,128)S(1)}, f32[2,1,16,256]{3,2,1,0:T(8,128)S(1)}, u32[]{:S(2)}, u32[]{:S(2)}) collective-permute-start(f32[2,1,16,256]{3,2,1,0:T(8,128)S(1)} %pad_maximum_fusion.10), channel_id=1, source_target_pairs={{8,0},{16,8},{24,16},{9,1},{17,9},{25,17},{10,2},{18,10},{26,18},{... | collective-permute-start | bytes 98312 | tf_op jit(solution)/shard_map/while/body/eval_jaxpr/ppermute | solution.py:15
  123.0 12.4 %collective-permute-start.2 = (f32[2,16,1,256]{3,2,1,0:T(1,128)S(1)}, f32[2,16,1,256]{3,2,1,0:T(1,128)S(1)}, u32[]{:S(2)}, u32[]{:S(2)}) collective-permute-start(f32[2,16,1,256]{3,2,1,0:T(1,128)S(1)} %pad_maximum_fusion.12), channel_id=1, source_target_pairs={{0,1},{1,2},{2,3},{3,4},{4,5},{5,6},{6,7},{8,9},{9,10},{10,11},{11... | collective-permute-start | bytes 98312 | tf_op jit(solution)/shard_map/while/body/eval_jaxpr/ppermute | solution.py:15
  144.4 9.9 %collective-permute-start.1 = (f32[2,16,1,256]{3,2,1,0:T(1,128)S(1)}, f32[2,16,1,256]{3,2,1,0:T(1,128)S(1)}, u32[]{:S(2)}, u32[]{:S(2)}) collective-permute-start(f32[2,16,1,256]{3,2,1,0:T(1,128)S(1)} %pad_maximum_fusion.11), channel_id=1, source_target_pairs={{1,0},{2,1},{3,2},{4,3},{5,4},{6,5},{7,6},{9,8},{10,9},{11,10},{12... | collective-permute-start | bytes 98312 | tf_op jit(solution)/shard_map/while/body/eval_jaxpr/ppermute | solution.py:15
  145.7 8.5 %collective-permute-start = (f32[2,1,16,256]{3,2,1,0:T(8,128)S(1)}, f32[2,1,16,256]{3,2,1,0:T(8,128)S(1)}, u32[]{:S(2)}, u32[]{:S(2)}) collective-permute-start(f32[2,1,16,256]{3,2,1,0:T(8,128)S(1)} %pad_maximum_fusion.10), channel_id=1, source_target_pairs={{8,0},{16,8},{24,16},{9,1},{17,9},{25,17},{10,2},{18,10},{26,18},{... | collective-permute-start | bytes 98312 | tf_op jit(solution)/shard_map/while/body/eval_jaxpr/ppermute | solution.py:15
  157.3 12.4 %collective-permute-start.2 = (f32[2,16,1,256]{3,2,1,0:T(1,128)S(1)}, f32[2,16,1,256]{3,2,1,0:T(1,128)S(1)}, u32[]{:S(2)}, u32[]{:S(2)}) collective-permute-start(f32[2,16,1,256]{3,2,1,0:T(1,128)S(1)} %pad_maximum_fusion.12), channel_id=1, source_target_pairs={{0,1},{1,2},{2,3},{3,4},{4,5},{5,6},{6,7},{8,9},{9,10},{10,11},{11... | collective-permute-start | bytes 98312 | tf_op jit(solution)/shard_map/while/body/eval_jaxpr/ppermute | solution.py:15
  178.7 9.9 %collective-permute-start.1 = (f32[2,16,1,256]{3,2,1,0:T(1,128)S(1)}, f32[2,16,1,256]{3,2,1,0:T(1,128)S(1)}, u32[]{:S(2)}, u32[]{:S(2)}) collective-permute-start(f32[2,16,1,256]{3,2,1,0:T(1,128)S(1)} %pad_maximum_fusion.11), channel_id=1, source_target_pairs={{1,0},{2,1},{3,2},{4,3},{5,4},{6,5},{7,6},{9,8},{10,9},{11,10},{12... | collective-permute-start | bytes 98312 | tf_op jit(solution)/shard_map/while/body/eval_jaxpr/ppermute | solution.py:15
  180.0 8.5 %collective-permute-start = (f32[2,1,16,256]{3,2,1,0:T(8,128)S(1)}, f32[2,1,16,256]{3,2,1,0:T(8,128)S(1)}, u32[]{:S(2)}, u32[]{:S(2)}) collective-permute-start(f32[2,1,16,256]{3,2,1,0:T(8,128)S(1)} %pad_maximum_fusion.10), channel_id=1, source_target_pairs={{8,0},{16,8},{24,16},{9,1},{17,9},{25,17},{10,2},{18,10},{26,18},{... | collective-permute-start | bytes 98312 | tf_op jit(solution)/shard_map/while/body/eval_jaxpr/ppermute | solution.py:15
  191.6 12.4 %collective-permute-start.2 = (f32[2,16,1,256]{3,2,1,0:T(1,128)S(1)}, f32[2,16,1,256]{3,2,1,0:T(1,128)S(1)}, u32[]{:S(2)}, u32[]{:S(2)}) collective-permute-start(f32[2,16,1,256]{3,2,1,0:T(1,128)S(1)} %pad_maximum_fusion.12), channel_id=1, source_target_pairs={{0,1},{1,2},{2,3},{3,4},{4,5},{5,6},{6,7},{8,9},{9,10},{10,11},{11... | collective-permute-start | bytes 98312 | tf_op jit(solution)/shard_map/while/body/eval_jaxpr/ppermute | solution.py:15
  213.0 9.9 %collective-permute-start.1 = (f32[2,16,1,256]{3,2,1,0:T(1,128)S(1)}, f32[2,16,1,256]{3,2,1,0:T(1,128)S(1)}, u32[]{:S(2)}, u32[]{:S(2)}) collective-permute-start(f32[2,16,1,256]{3,2,1,0:T(1,128)S(1)} %pad_maximum_fusion.11), channel_id=1, source_target_pairs={{1,0},{2,1},{3,2},{4,3},{5,4},{6,5},{7,6},{9,8},{10,9},{11,10},{12... | collective-permute-start | bytes 98312 | tf_op jit(solution)/shard_map/while/body/eval_jaxpr/ppermute | solution.py:15
  214.3 8.5 %collective-permute-start = (f32[2,1,16,256]{3,2,1,0:T(8,128)S(1)}, f32[2,1,16,256]{3,2,1,0:T(8,128)S(1)}, u32[]{:S(2)}, u32[]{:S(2)}) collective-permute-start(f32[2,1,16,256]{3,2,1,0:T(8,128)S(1)} %pad_maximum_fusion.10), channel_id=1, source_target_pairs={{8,0},{16,8},{24,16},{9,1},{17,9},{25,17},{10,2},{18,10},{26,18},{... | collective-permute-start | bytes 98312 | tf_op jit(solution)/shard_map/while/body/eval_jaxpr/ppermute | solution.py:15
  225.9 12.4 %collective-permute-start.2 = (f32[2,16,1,256]{3,2,1,0:T(1,128)S(1)}, f32[2,16,1,256]{3,2,1,0:T(1,128)S(1)}, u32[]{:S(2)}, u32[]{:S(2)}) collective-permute-start(f32[2,16,1,256]{3,2,1,0:T(1,128)S(1)} %pad_maximum_fusion.12), channel_id=1, source_target_pairs={{0,1},{1,2},{2,3},{3,4},{4,5},{5,6},{6,7},{8,9},{9,10},{10,11},{11... | collective-permute-start | bytes 98312 | tf_op jit(solution)/shard_map/while/body/eval_jaxpr/ppermute | solution.py:15
  247.3 9.9 %collective-permute-start.1 = (f32[2,16,1,256]{3,2,1,0:T(1,128)S(1)}, f32[2,16,1,256]{3,2,1,0:T(1,128)S(1)}, u32[]{:S(2)}, u32[]{:S(2)}) collective-permute-start(f32[2,16,1,256]{3,2,1,0:T(1,128)S(1)} %pad_maximum_fusion.11), channel_id=1, source_target_pairs={{1,0},{2,1},{3,2},{4,3},{5,4},{6,5},{7,6},{9,8},{10,9},{11,10},{12... | collective-permute-start | bytes 98312 | tf_op jit(solution)/shard_map/while/body/eval_jaxpr/ppermute | solution.py:15
  248.6 8.5 %collective-permute-start = (f32[2,1,16,256]{3,2,1,0:T(8,128)S(1)}, f32[2,1,16,256]{3,2,1,0:T(8,128)S(1)}, u32[]{:S(2)}, u32[]{:S(2)}) collective-permute-start(f32[2,1,16,256]{3,2,1,0:T(8,128)S(1)} %pad_maximum_fusion.10), channel_id=1, source_target_pairs={{8,0},{16,8},{24,16},{9,1},{17,9},{25,17},{10,2},{18,10},{26,18},{... | collective-permute-start | bytes 98312 | tf_op jit(solution)/shard_map/while/body/eval_jaxpr/ppermute | solution.py:15
  260.2 12.4 %collective-permute-start.2 = (f32[2,16,1,256]{3,2,1,0:T(1,128)S(1)}, f32[2,16,1,256]{3,2,1,0:T(1,128)S(1)}, u32[]{:S(2)}, u32[]{:S(2)}) collective-permute-start(f32[2,16,1,256]{3,2,1,0:T(1,128)S(1)} %pad_maximum_fusion.12), channel_id=1, source_target_pairs={{0,1},{1,2},{2,3},{3,4},{4,5},{5,6},{6,7},{8,9},{9,10},{10,11},{11... | collective-permute-start | bytes 98312 | tf_op jit(solution)/shard_map/while/body/eval_jaxpr/ppermute | solution.py:15
  281.6 9.9 %collective-permute-start.1 = (f32[2,16,1,256]{3,2,1,0:T(1,128)S(1)}, f32[2,16,1,256]{3,2,1,0:T(1,128)S(1)}, u32[]{:S(2)}, u32[]{:S(2)}) collective-permute-start(f32[2,16,1,256]{3,2,1,0:T(1,128)S(1)} %pad_maximum_fusion.11), channel_id=1, source_target_pairs={{1,0},{2,1},{3,2},{4,3},{5,4},{6,5},{7,6},{9,8},{10,9},{11,10},{12... | collective-permute-start | bytes 98312 | tf_op jit(solution)/shard_map/while/body/eval_jaxpr/ppermute | solution.py:15
  282.9 8.5 %collective-permute-start = (f32[2,1,16,256]{3,2,1,0:T(8,128)S(1)}, f32[2,1,16,256]{3,2,1,0:T(8,128)S(1)}, u32[]{:S(2)}, u32[]{:S(2)}) collective-permute-start(f32[2,1,16,256]{3,2,1,0:T(8,128)S(1)} %pad_maximum_fusion.10), channel_id=1, source_target_pairs={{8,0},{16,8},{24,16},{9,1},{17,9},{25,17},{10,2},{18,10},{26,18},{... | collective-permute-start | bytes 98312 | tf_op jit(solution)/shard_map/while/body/eval_jaxpr/ppermute | solution.py:15
  294.5 12.4 %collective-permute-start.2 = (f32[2,16,1,256]{3,2,1,0:T(1,128)S(1)}, f32[2,16,1,256]{3,2,1,0:T(1,128)S(1)}, u32[]{:S(2)}, u32[]{:S(2)}) collective-permute-start(f32[2,16,1,256]{3,2,1,0:T(1,128)S(1)} %pad_maximum_fusion.12), channel_id=1, source_target_pairs={{0,1},{1,2},{2,3},{3,4},{4,5},{5,6},{6,7},{8,9},{9,10},{10,11},{11... | collective-permute-start | bytes 98312 | tf_op jit(solution)/shard_map/while/body/eval_jaxpr/ppermute | solution.py:15
  315.9 9.9 %collective-permute-start.1 = (f32[2,16,1,256]{3,2,1,0:T(1,128)S(1)}, f32[2,16,1,256]{3,2,1,0:T(1,128)S(1)}, u32[]{:S(2)}, u32[]{:S(2)}) collective-permute-start(f32[2,16,1,256]{3,2,1,0:T(1,128)S(1)} %pad_maximum_fusion.11), channel_id=1, source_target_pairs={{1,0},{2,1},{3,2},{4,3},{5,4},{6,5},{7,6},{9,8},{10,9},{11,10},{12... | collective-permute-start | bytes 98312 | tf_op jit(solution)/shard_map/while/body/eval_jaxpr/ppermute | solution.py:15
  317.2 8.5 %collective-permute-start = (f32[2,1,16,256]{3,2,1,0:T(8,128)S(1)}, f32[2,1,16,256]{3,2,1,0:T(8,128)S(1)}, u32[]{:S(2)}, u32[]{:S(2)}) collective-permute-start(f32[2,1,16,256]{3,2,1,0:T(8,128)S(1)} %pad_maximum_fusion.10), channel_id=1, source_target_pairs={{8,0},{16,8},{24,16},{9,1},{17,9},{25,17},{10,2},{18,10},{26,18},{... | collective-permute-start | bytes 98312 | tf_op jit(solution)/shard_map/while/body/eval_jaxpr/ppermute | solution.py:15
  328.8 12.4 %collective-permute-start.2 = (f32[2,16,1,256]{3,2,1,0:T(1,128)S(1)}, f32[2,16,1,256]{3,2,1,0:T(1,128)S(1)}, u32[]{:S(2)}, u32[]{:S(2)}) collective-permute-start(f32[2,16,1,256]{3,2,1,0:T(1,128)S(1)} %pad_maximum_fusion.12), channel_id=1, source_target_pairs={{0,1},{1,2},{2,3},{3,4},{4,5},{5,6},{6,7},{8,9},{9,10},{10,11},{11... | collective-permute-start | bytes 98312 | tf_op jit(solution)/shard_map/while/body/eval_jaxpr/ppermute | solution.py:15
  350.2 9.9 %collective-permute-start.1 = (f32[2,16,1,256]{3,2,1,0:T(1,128)S(1)}, f32[2,16,1,256]{3,2,1,0:T(1,128)S(1)}, u32[]{:S(2)}, u32[]{:S(2)}) collective-permute-start(f32[2,16,1,256]{3,2,1,0:T(1,128)S(1)} %pad_maximum_fusion.11), channel_id=1, source_target_pairs={{1,0},{2,1},{3,2},{4,3},{5,4},{6,5},{7,6},{9,8},{10,9},{11,10},{12... | collective-permute-start | bytes 98312 | tf_op jit(solution)/shard_map/while/body/eval_jaxpr/ppermute | solution.py:15
  351.5 8.5 %collective-permute-start = (f32[2,1,16,256]{3,2,1,0:T(8,128)S(1)}, f32[2,1,16,256]{3,2,1,0:T(8,128)S(1)}, u32[]{:S(2)}, u32[]{:S(2)}) collective-permute-start(f32[2,1,16,256]{3,2,1,0:T(8,128)S(1)} %pad_maximum_fusion.10), channel_id=1, source_target_pairs={{8,0},{16,8},{24,16},{9,1},{17,9},{25,17},{10,2},{18,10},{26,18},{... | collective-permute-start | bytes 98312 | tf_op jit(solution)/shard_map/while/body/eval_jaxpr/ppermute | solution.py:15
  363.1 12.4 %collective-permute-start.2 = (f32[2,16,1,256]{3,2,1,0:T(1,128)S(1)}, f32[2,16,1,256]{3,2,1,0:T(1,128)S(1)}, u32[]{:S(2)}, u32[]{:S(2)}) collective-permute-start(f32[2,16,1,256]{3,2,1,0:T(1,128)S(1)} %pad_maximum_fusion.12), channel_id=1, source_target_pairs={{0,1},{1,2},{2,3},{3,4},{4,5},{5,6},{6,7},{8,9},{9,10},{10,11},{11... | collective-permute-start | bytes 98312 | tf_op jit(solution)/shard_map/while/body/eval_jaxpr/ppermute | solution.py:15
  384.5 9.9 %collective-permute-start.1 = (f32[2,16,1,256]{3,2,1,0:T(1,128)S(1)}, f32[2,16,1,256]{3,2,1,0:T(1,128)S(1)}, u32[]{:S(2)}, u32[]{:S(2)}) collective-permute-start(f32[2,16,1,256]{3,2,1,0:T(1,128)S(1)} %pad_maximum_fusion.11), channel_id=1, source_target_pairs={{1,0},{2,1},{3,2},{4,3},{5,4},{6,5},{7,6},{9,8},{10,9},{11,10},{12... | collective-permute-start | bytes 98312 | tf_op jit(solution)/shard_map/while/body/eval_jaxpr/ppermute | solution.py:15
  385.8 8.5 %collective-permute-start = (f32[2,1,16,256]{3,2,1,0:T(8,128)S(1)}, f32[2,1,16,256]{3,2,1,0:T(8,128)S(1)}, u32[]{:S(2)}, u32[]{:S(2)}) collective-permute-start(f32[2,1,16,256]{3,2,1,0:T(8,128)S(1)} %pad_maximum_fusion.10), channel_id=1, source_target_pairs={{8,0},{16,8},{24,16},{9,1},{17,9},{25,17},{10,2},{18,10},{26,18},{... | collective-permute-start | bytes 98312 | tf_op jit(solution)/shard_map/while/body/eval_jaxpr/ppermute | solution.py:15
  397.4 12.4 %collective-permute-start.2 = (f32[2,16,1,256]{3,2,1,0:T(1,128)S(1)}, f32[2,16,1,256]{3,2,1,0:T(1,128)S(1)}, u32[]{:S(2)}, u32[]{:S(2)}) collective-permute-start(f32[2,16,1,256]{3,2,1,0:T(1,128)S(1)} %pad_maximum_fusion.12), channel_id=1, source_target_pairs={{0,1},{1,2},{2,3},{3,4},{4,5},{5,6},{6,7},{8,9},{9,10},{10,11},{11... | collective-permute-start | bytes 98312 | tf_op jit(solution)/shard_map/while/body/eval_jaxpr/ppermute | solution.py:15
  418.8 9.9 %collective-permute-start.1 = (f32[2,16,1,256]{3,2,1,0:T(1,128)S(1)}, f32[2,16,1,256]{3,2,1,0:T(1,128)S(1)}, u32[]{:S(2)}, u32[]{:S(2)}) collective-permute-start(f32[2,16,1,256]{3,2,1,0:T(1,128)S(1)} %pad_maximum_fusion.11), channel_id=1, source_target_pairs={{1,0},{2,1},{3,2},{4,3},{5,4},{6,5},{7,6},{9,8},{10,9},{11,10},{12... | collective-permute-start | bytes 98312 | tf_op jit(solution)/shard_map/while/body/eval_jaxpr/ppermute | solution.py:15
  420.1 8.5 %collective-permute-start = (f32[2,1,16,256]{3,2,1,0:T(8,128)S(1)}, f32[2,1,16,256]{3,2,1,0:T(8,128)S(1)}, u32[]{:S(2)}, u32[]{:S(2)}) collective-permute-start(f32[2,1,16,256]{3,2,1,0:T(8,128)S(1)} %pad_maximum_fusion.10), channel_id=1, source_target_pairs={{8,0},{16,8},{24,16},{9,1},{17,9},{25,17},{10,2},{18,10},{26,18},{... | collective-permute-start | bytes 98312 | tf_op jit(solution)/shard_map/while/body/eval_jaxpr/ppermute | solution.py:15
  431.7 12.4 %collective-permute-start.2 = (f32[2,16,1,256]{3,2,1,0:T(1,128)S(1)}, f32[2,16,1,256]{3,2,1,0:T(1,128)S(1)}, u32[]{:S(2)}, u32[]{:S(2)}) collective-permute-start(f32[2,16,1,256]{3,2,1,0:T(1,128)S(1)} %pad_maximum_fusion.12), channel_id=1, source_target_pairs={{0,1},{1,2},{2,3},{3,4},{4,5},{5,6},{6,7},{8,9},{9,10},{10,11},{11... | collective-permute-start | bytes 98312 | tf_op jit(solution)/shard_map/while/body/eval_jaxpr/ppermute | solution.py:15
  453.1 9.9 %collective-permute-start.1 = (f32[2,16,1,256]{3,2,1,0:T(1,128)S(1)}, f32[2,16,1,256]{3,2,1,0:T(1,128)S(1)}, u32[]{:S(2)}, u32[]{:S(2)}) collective-permute-start(f32[2,16,1,256]{3,2,1,0:T(1,128)S(1)} %pad_maximum_fusion.11), channel_id=1, source_target_pairs={{1,0},{2,1},{3,2},{4,3},{5,4},{6,5},{7,6},{9,8},{10,9},{11,10},{12... | collective-permute-start | bytes 98312 | tf_op jit(solution)/shard_map/while/body/eval_jaxpr/ppermute | solution.py:15
  454.4 8.5 %collective-permute-start = (f32[2,1,16,256]{3,2,1,0:T(8,128)S(1)}, f32[2,1,16,256]{3,2,1,0:T(8,128)S(1)}, u32[]{:S(2)}, u32[]{:S(2)}) collective-permute-start(f32[2,1,16,256]{3,2,1,0:T(8,128)S(1)} %pad_maximum_fusion.10), channel_id=1, source_target_pairs={{8,0},{16,8},{24,16},{9,1},{17,9},{25,17},{10,2},{18,10},{26,18},{... | collective-permute-start | bytes 98312 | tf_op jit(solution)/shard_map/while/body/eval_jaxpr/ppermute | solution.py:15
  466.0 12.4 %collective-permute-start.2 = (f32[2,16,1,256]{3,2,1,0:T(1,128)S(1)}, f32[2,16,1,256]{3,2,1,0:T(1,128)S(1)}, u32[]{:S(2)}, u32[]{:S(2)}) collective-permute-start(f32[2,16,1,256]{3,2,1,0:T(1,128)S(1)} %pad_maximum_fusion.12), channel_id=1, source_target_pairs={{0,1},{1,2},{2,3},{3,4},{4,5},{5,6},{6,7},{8,9},{9,10},{10,11},{11... | collective-permute-start | bytes 98312 | tf_op jit(solution)/shard_map/while/body/eval_jaxpr/ppermute | solution.py:15
  487.4 9.9 %collective-permute-start.1 = (f32[2,16,1,256]{3,2,1,0:T(1,128)S(1)}, f32[2,16,1,256]{3,2,1,0:T(1,128)S(1)}, u32[]{:S(2)}, u32[]{:S(2)}) collective-permute-start(f32[2,16,1,256]{3,2,1,0:T(1,128)S(1)} %pad_maximum_fusion.11), channel_id=1, source_target_pairs={{1,0},{2,1},{3,2},{4,3},{5,4},{6,5},{7,6},{9,8},{10,9},{11,10},{12... | collective-permute-start | bytes 98312 | tf_op jit(solution)/shard_map/while/body/eval_jaxpr/ppermute | solution.py:15
  488.7 8.5 %collective-permute-start = (f32[2,1,16,256]{3,2,1,0:T(8,128)S(1)}, f32[2,1,16,256]{3,2,1,0:T(8,128)S(1)}, u32[]{:S(2)}, u32[]{:S(2)}) collective-permute-start(f32[2,1,16,256]{3,2,1,0:T(8,128)S(1)} %pad_maximum_fusion.10), channel_id=1, source_target_pairs={{8,0},{16,8},{24,16},{9,1},{17,9},{25,17},{10,2},{18,10},{26,18},{... | collective-permute-start | bytes 98312 | tf_op jit(solution)/shard_map/while/body/eval_jaxpr/ppermute | solution.py:15
  500.3 12.4 %collective-permute-start.2 = (f32[2,16,1,256]{3,2,1,0:T(1,128)S(1)}, f32[2,16,1,256]{3,2,1,0:T(1,128)S(1)}, u32[]{:S(2)}, u32[]{:S(2)}) collective-permute-start(f32[2,16,1,256]{3,2,1,0:T(1,128)S(1)} %pad_maximum_fusion.12), channel_id=1, source_target_pairs={{0,1},{1,2},{2,3},{3,4},{4,5},{5,6},{6,7},{8,9},{9,10},{10,11},{11... | collective-permute-start | bytes 98312 | tf_op jit(solution)/shard_map/while/body/eval_jaxpr/ppermute | solution.py:15
  521.7 9.9 %collective-permute-start.1 = (f32[2,16,1,256]{3,2,1,0:T(1,128)S(1)}, f32[2,16,1,256]{3,2,1,0:T(1,128)S(1)}, u32[]{:S(2)}, u32[]{:S(2)}) collective-permute-start(f32[2,16,1,256]{3,2,1,0:T(1,128)S(1)} %pad_maximum_fusion.11), channel_id=1, source_target_pairs={{1,0},{2,1},{3,2},{4,3},{5,4},{6,5},{7,6},{9,8},{10,9},{11,10},{12... | collective-permute-start | bytes 98312 | tf_op jit(solution)/shard_map/while/body/eval_jaxpr/ppermute | solution.py:15
  523.0 8.5 %collective-permute-start = (f32[2,1,16,256]{3,2,1,0:T(8,128)S(1)}, f32[2,1,16,256]{3,2,1,0:T(8,128)S(1)}, u32[]{:S(2)}, u32[]{:S(2)}) collective-permute-start(f32[2,1,16,256]{3,2,1,0:T(8,128)S(1)} %pad_maximum_fusion.10), channel_id=1, source_target_pairs={{8,0},{16,8},{24,16},{9,1},{17,9},{25,17},{10,2},{18,10},{26,18},{... | collective-permute-start | bytes 98312 | tf_op jit(solution)/shard_map/while/body/eval_jaxpr/ppermute | solution.py:15
  534.6 12.4 %collective-permute-start.2 = (f32[2,16,1,256]{3,2,1,0:T(1,128)S(1)}, f32[2,16,1,256]{3,2,1,0:T(1,128)S(1)}, u32[]{:S(2)}, u32[]{:S(2)}) collective-permute-start(f32[2,16,1,256]{3,2,1,0:T(1,128)S(1)} %pad_maximum_fusion.12), channel_id=1, source_target_pairs={{0,1},{1,2},{2,3},{3,4},{4,5},{5,6},{6,7},{8,9},{9,10},{10,11},{11... | collective-permute-start | bytes 98312 | tf_op jit(solution)/shard_map/while/body/eval_jaxpr/ppermute | solution.py:15
  (440 other events, 2458.9 us)
where the time goes:
time: 612 us; the launch traced here: 605 us
  starting transfers between devices  205 us (33%)
  local copies, waits for them, and re-layouts  160 us (26%)
  other arithmetic  119 us (19%)
  matrix products  52.2 us (9%)
  blocking collectives  45.9 us (8%)
  waiting for transfers between devices  13.2 us (2%)
  loops' own time  7.44 us (1%)
    ppermute x64, starting transfers between devices, passed_along(): return lax.ppermute(block, axis, route)  205 us
    slice x96, local copies, waits for them, and re-layouts, difference(): lax.slice_in_dim(values, 1, length, axis=axis)  73.3 us
    sub x48, other arithmetic, turn_parts(): field_h[number] - courant * rotation[number]  50.2 us
    psum x1, blocking collectives, local(): port_power = lax.psum(partial_value, ('gx', 'gy'))  45.9 us
    add x16, other arithmetic, turn_parts(): field_e[1] + factor * rotation[1]  38.7 us
    while x832, local copies, waits for them, and re-layouts  36.9 us
    dot_general x16, matrix products, inject(): lax.dot_general(weighted, depth_table, (((0,), (0,)), ((), ())), precisio...  30.5 us
    dynamic_update_slice x16, local copies, waits for them, and re-layouts, note_power(): return lax.dynamic_update_slice_in_dim(record, drive[None, :], index, 0)  21.4 us
  transfers between devices with their start and end apart: 64, of which 16 were waited for; matrix products, arithmetic and copies ran while one was open for 22% of the time, Pallas kernels for 0%

commit v1 on v0

v1 whole, which is shorter than its diff:
```python
import functools

import jax
import jax.numpy as jnp
from jax import lax
from jax.experimental import pallas as pl
from jax.experimental.pallas import tpu as pltpu
from jax.sharding import PartitionSpec as P

courant = 0.55
absorb_keep = (0.0, 0.92, 0.75, 0.45)
absorb_take = (0.0, -0.06, -0.18, -0.35)
pairs = ((2, 1), (1, 2), (0, 2), (2, 0), (1, 0), (0, 1))

vmem_spec = pl.BlockSpec(memory_space=pltpu.VMEM)


def passed_along(block, axis, distance):
    devices = range(lax.axis_size(axis))
    route = [(i - distance, i) for i in devices if i - distance in devices]
    return lax.ppermute(block, axis, route)


def grade_table(grades, table):
    result = jnp.zeros(grades.shape, jnp.float32)
    for level in range(1, 4):
        result = result + jnp.where(grades == level, table[level], 0.0)
    return result


def fixed(x):
    return pltpu.with_memory_space_constraint(x, pltpu.VMEM)


def call(body, args, pinned, outs, aliases, limit=6 << 20):
    args = [fixed(a) if i in pinned else a for i, a in enumerate(args)]
    shapes = [
        pltpu.VMEM(s, d) if keep else jax.ShapeDtypeStruct(s, d) for s, d, keep in outs
    ]
    return pl.pallas_call(
        body,
        out_shape=shapes,
        in_specs=[vmem_spec] * len(args),
        out_specs=[vmem_spec] * len(outs),
        input_output_aliases=aliases,
        compiler_params=pltpu.CompilerParams(vmem_limit_bytes=limit),
    )(*args)


def shifted(v, axis, forward, inner):
    n = v.shape[axis]
    rolled = pltpu.roll(v, n - 1 if forward else 1, axis)
    return jnp.where(inner, rolled, 0.0)


def main_kernel(forward, *refs):
    if forward:
        src, dst, mem, keep, take, dst_o, mem_o = refs
    else:
        src, dst, mem, keep, take, factor, source, dst_o, mem_o = refs
    _, nx, ny, nz = src.shape
    row = lax.broadcasted_iota(jnp.int32, (ny, nz), 0)
    col = lax.broadcasted_iota(jnp.int32, (ny, nz), 1)
    inner_y = row < ny - 1 if forward else row > 0
    inner_z = col < nz - 1 if forward else col > 0

    def plane(x, _):
        if forward:
            beside = jnp.minimum(x + 1, nx - 1)
            valid = (x < nx - 1).astype(jnp.float32)
        else:
            beside = jnp.maximum(x - 1, 0)
            valid = (x > 0).astype(jnp.float32)
        here = [src[c, x] for c in range(3)]
        kept = [keep[d, x] for d in range(3)]
        taken = [take[d, x] for d in range(3)]
        terms = []
        for k, (c, d) in enumerate(pairs):
            if d == 0:
                other = src[c, beside] * valid
            elif d == 1:
                other = shifted(here[c], 0, forward, inner_y)
            else:
                other = shifted(here[c], 1, forward, inner_z)
            slope = other - here[c] if forward else here[c] - other
            carried = kept[d] * mem[k, x] + taken[d] * slope
            mem_o[k, x] = carried
            terms.append(slope + carried)
        for c in range(3):
            rotation = terms[2 * c] - terms[2 * c + 1]
            if forward:
                dst_o[c, x] = dst[c, x] - courant * rotation
            else:
                value = dst[c, x] + factor[x] * rotation
                if c == 2:
                    value = value - source[x]
                dst_o[c, x] = value
        return 0

    lax.fori_loop(0, nx, plane, 0, unroll=2)


def edge_kernel(forward, *refs):
    if forward:
        dst, mem, take, px, py, dst_o, mem_o, sx, sy = refs
        weight = lambda x, ys: -courant
        sign = 1.0
    else:
        dst, mem, take, factor, px, py, dst_o, mem_o, sx, sy = refs
        weight = lambda x, ys: factor[x, ys]
        sign = -1.0
    _, nx, ny, nz = dst.shape
    x = nx - 1 if forward else 0
    whole = slice(None)
    taken = take[0, x]
    scale = weight(x, whole) * sign
    for k, p in ((3, 1), (4, 0)):
        part = taken * px[p]
        mem_o[k, x] = mem[k, x] + sign * part
        grown = scale * (px[p] + part)
        c = k // 2
        if k == 3:
            dst_o[c, x] = dst[c, x] - grown
        else:
            dst_o[c, x] = dst[c, x] + grown
    y = ny - 1 if forward else 0
    ys = slice(y, y + 1)
    for i in range(nx):
        taken = take[1, i, ys]
        scale = weight(i, ys) * sign
        for k, p in ((0, 1), (5, 0)):
            part = taken * py[p, i:i + 1]
            mem_o[k, i, ys] = mem[k, i, ys] + sign * part
            grown = scale * (py[p, i:i + 1] + part)
            c = k // 2
            base = dst_o if (k == 5 and i == x) else dst
            if k == 0:
                fresh = base[c, i, ys] + grown
            else:
                fresh = base[c, i, ys] - grown
            dst_o[c, i, ys] = fresh
            sy[c // 2, i:i + 1] = fresh
    sx[0] = dst_o[1, x]
    sx[1] = dst_o[2, x]


def halves(values):
    high = values.astype(jnp.bfloat16)
    return high, (values - high.astype(jnp.float32)).astype(jnp.bfloat16)


def source_of(cell_t, depth, pushed):
    high, low = halves(pushed)
    top = jnp.dot(cell_t * high, depth, preferred_element_type=jnp.float32)
    return top + jnp.dot(cell_t * low, depth, preferred_element_type=jnp.float32)


def dipole_kernel(step, last, *refs):
    refs = list(refs)
    first = step == 0
    if not first:
        field, cell = refs[0:2]
        refs = refs[2:]
    depth = refs[0]
    refs = refs[1:]
    if not last:
        cell_t, pushed = refs[0:2]
        refs = refs[2:]
    if not first:
        _, nx, ny, nz = field.shape
        values = field[2].reshape(nx * ny, nz)
        top, rest = halves(values)
        picked = jnp.dot(cell[...], top, preferred_element_type=jnp.float32)
        picked = picked + jnp.dot(cell[...], rest, preferred_element_type=jnp.float32)
        refs[0][...] = jnp.sum(picked * depth[...].astype(jnp.float32), axis=1, keepdims=True)
        refs = refs[1:]
    if not last:
        out = refs[0]
        out[...] = source_of(cell_t[...], depth[...], pushed[step:step + 1]).reshape(out.shape)


def summed(values, axis):
    size = lax.axis_size(axis)
    if size & (size - 1):
        return lax.psum(values, axis)
    distance = 1
    while distance < size:
        values = values + lax.ppermute(values, axis, [(i, i ^ distance) for i in range(size)])
        distance *= 2
    return values


def local(
    electric,
    magnetic,
    aux_electric,
    aux_magnetic,
    grades,
    permittivity,
    dipole_cell,
    dipole_port,
    live_count,
    injection,
    waveform,
):
    nx, ny, nz = electric.shape[1:]
    slots = dipole_cell.shape[1]
    ports, steps = waveform.shape
    f32 = jnp.float32
    row_index = lax.axis_index("gx")
    col_index = lax.axis_index("gy")
    plane_cell = (dipole_cell[0] - row_index * nx) * ny + (dipole_cell[1] - col_index * ny)
    cells = jnp.arange(nx * ny, dtype=jnp.int32)
    cell = (plane_cell[:, None] == cells[None, :]).astype(jnp.bfloat16)
    cell_t = (cells[:, None] == plane_cell[None, :]).astype(jnp.bfloat16)
    depth = (dipole_cell[2][:, None] == jnp.arange(nz, dtype=jnp.int32)[None, :]).astype(
        jnp.bfloat16
    )
    live = (jnp.arange(slots, dtype=jnp.int32) < live_count[0]).astype(f32)
    current = jnp.dot(injection, waveform, preferred_element_type=f32) * live[:, None]
    pushed = courant * current.T
    members = (dipole_port[:, None] == jnp.arange(ports, dtype=jnp.int32)[None, :]).astype(f32)
    factor = courant / permittivity
    keep = grade_table(grades, absorb_keep)
    take = grade_table(grades, absorb_take)

    field = (3, nx, ny, nz)
    memory = (6, nx, ny, nz)
    block = (nx, ny, nz)
    send_x = ((2, ny, nz), f32, False)
    send_y = ((2, nx, nz), f32, False)
    state = [(field, f32, True), (memory, f32, True)]
    picks = []
    (source,) = call(
        functools.partial(dipole_kernel, 0, False),
        [depth, cell_t, pushed],
        range(3),
        [(block, f32, True)],
        {},
    )
    sx = jnp.stack([electric[1, 0], electric[2, 0]])
    sy = jnp.stack([electric[0, :, 0], electric[2, :, 0]])
    for step in range(steps):
        px = passed_along(sx, "gx", -1)
        py = passed_along(sy, "gy", -1)
        magnetic, aux_electric = call(
            functools.partial(main_kernel, True),
            [electric, magnetic, aux_electric, keep, take],
            range(5),
            state,
            {1: 0, 2: 1},
        )
        magnetic, aux_electric, sx, sy = call(
            functools.partial(edge_kernel, True),
            [magnetic, aux_electric, take, px, py],
            range(3),
            state + [send_x, send_y],
            {0: 0, 1: 1},
        )
        px = passed_along(sx, "gx", 1)
        py = passed_along(sy, "gy", 1)
        electric, aux_magnetic = call(
            functools.partial(main_kernel, False),
            [magnetic, electric, aux_magnetic, keep, take, factor, source],
            range(7),
            state,
            {1: 0, 2: 1},
        )
        electric, aux_magnetic, sx, sy = call(
            functools.partial(edge_kernel, False),
            [electric, aux_magnetic, take, factor, px, py],
            range(4),
            state + [send_x, send_y],
            {0: 0, 1: 1},
        )
        last = step == steps - 1
        args = [electric, cell, depth]
        outs = [((slots, 1), f32, False)]
        if not last:
            args += [cell_t, pushed]
            outs.append((block, f32, True))
        results = call(
            functools.partial(dipole_kernel, step + 1, last), args, range(len(args)), outs, {}
        )
        picks.append(results[0])
        if not last:
            source = results[1]
    record = jnp.concatenate(picks, axis=1) * current
    partial_value = lax.dot_general(
        record, members, (((0,), (0,)), ((), ())), precision=lax.Precision.HIGHEST
    )
    port_power = summed(summed(partial_value, "gx"), "gy")
    return (electric, magnetic, port_power)


def solution(mesh):
    in_specs = (
        P(None, "gx", "gy", None),
        P(None, "gx", "gy", None),
        P(None, "gx", "gy", None),
        P(None, "gx", "gy", None),
        P(None, "gx", "gy", None),
        P("gx", "gy", None),
        P(None, ("gx", "gy")),
        P(("gx", "gy")),
        P(("gx", "gy")),
        P(("gx", "gy"), None),
        P(),
    )
    out_specs = (P(None, "gx", "gy", None), P(None, "gx", "gy", None), P())
    return jax.shard_map(local, mesh=mesh, in_specs=in_specs, out_specs=out_specs, check_vma=False)
```

time: 612 us -> 336 us (0.55)
  local copies, waits for them, and re-layouts: 160 us -> 37.4 us
  other arithmetic: 119 us -> 1.79 us
  matrix products: 52.2 us -> 0.72 us
  waiting for transfers between devices: 13.2 us -> 63.5 us
  Pallas kernels: 0 us -> 49.7 us
  blocking collectives: 45.9 us -> 0 us
  starting transfers between devices: 205 us -> 178 us
  loops' own time: 7.44 us -> 0 us
    slice x128 -> x1, local copies, waits for them, and re-layouts: 84.8 us -> 0.02 us  [local(): sy = jnp.stack([electric[0, :, 0], electric[2, :, 0]])]
    sub x64 -> x0, other arithmetic: 56.9 us -> none  [the longest x48 50.2 us: turn_parts(): field_h[number] - courant * rotation[number]]
    dot_general x34 -> x2, matrix products: 52.2 us -> 0.72 us  [the longest x1 0.49 us: local(): lax.dot_general(record, members, (((0,), (0,)), ((), ())), precision=lax....]
    pallas_call x0 -> x81, Pallas kernels: none -> 49.7 us  [call(): pl.pallas_call(body, out_shape=shapes, in_specs=[vmem_spec] * len(args),...]
    psum x1 -> x0, blocking collectives: 45.9 us -> none  [local(): port_power = lax.psum(partial_value, ('gx', 'gy'))]
    add x32 -> x6, other arithmetic: 44.3 us -> 0.66 us  [the longest x5 0.65 us: summed(): values + lax.ppermute(values, axis, [(i, i ^ distance) for i in range(siz...]
    ppermute x64, waiting for transfers between devices: 13.2 us -> 53.7 us  [passed_along(): return lax.ppermute(block, axis, route)]
    while x832 -> x0, local copies, waits for them, and re-layouts: 36.9 us -> none
  transfers between devices with their start and end apart: 64 -> 69, of which waited for: 16 -> 36; matrix products, arithmetic and copies ran while one was open for 22% -> 8% of each run, Pallas kernels for 0% -> 13%
where the time goes in v1:
time: 336 us; the launch traced here: 334 us
  starting transfers between devices  178 us (53%)
  waiting for transfers between devices  63.5 us (19%)
  Pallas kernels  49.7 us (15%)
  local copies, waits for them, and re-layouts  37.4 us (11%)
    ppermute x64, starting transfers between devices, passed_along(): return lax.ppermute(block, axis, route)  169 us
    ppermute x64, waiting for transfers between devices, passed_along(): return lax.ppermute(block, axis, route)  53.7 us
    pallas_call x81, Pallas kernels, call(): pl.pallas_call(body, out_shape=shapes, in_specs=[vmem_spec] * len(args),...  49.7 us
    pallas_call x16, local copies, waits for them, and re-layouts, call(): pl.pallas_call(body, out_shape=shapes, in_specs=[vmem_spec] * len(args),...  22.4 us
    unnamed x106, local copies, waits for them, and re-layouts  14.9 us
    ppermute x5, waiting for transfers between devices, summed(): lax.ppermute(values, axis, [(i, i ^ distance) for i in range(size)])  9.76 us
    ppermute x5, starting transfers between devices, summed(): lax.ppermute(values, axis, [(i, i ^ distance) for i in range(size)])  8.52 us
  transfers between devices with their start and end apart: 69, of which 36 were waited for; matrix products, arithmetic and copies ran while one was open for 8% of the time, Pallas kernels for 13%

profile of v1, /device:TPU:0, one launch (start us, length us, event | category | flops | bytes accessed | tf_op | source)
XLA Modules:
  0.0 333.8 jit_solution(10680622922273200015)
XLA Ops:
  0.7 2.9 copy.318.refs_2_
  12.8 3.2 collective-permute-start.2
  16.0 5.5 %collective-permute-start.3 = (f32[2,16,256]{2,1,0:T(8,128)S(1)}, f32[2,16,256]{2,1,0:T(8,128)S(1)}, u32[]{:S(2)}, u32[]{:S(2)}) collective-permute-start(f32[2,16,256]{2,1,0:T(8,128)S(1)} %get-tuple-element.227), channel_id=1, source_target_pairs={{0,1},{1,2},{2,3},{3,4},{4,5},{5,6},{6,7},{8,9},{9,10},{10,11},{11... | collective-permute-start | bytes 98312 | tf_op jit(solution)/shard_map/ppermute | solution.py:21
  27.1 4.2 %collective-permute-done.5.refs_4_ = f32[2,16,256]{2,1,0:T(8,128)S(1)} collective-permute-done((f32[2,16,256]{2,1,0:T(8,128)S(1)}, f32[2,16,256]{2,1,0:T(8,128)S(1)}, u32[]{:S(2)}, u32[]{:S(2)}) %collective-permute-start.5) | collective-permute-done | bytes 32800 | tf_op jit(solution)/shard_map/ppermute | solution.py:21
  31.4 2.4 collective-permute-start.6
  33.8 5.1 %collective-permute-start.7 = (f32[2,16,256]{2,1,0:T(8,128)S(1)}, f32[2,16,256]{2,1,0:T(8,128)S(1)}, u32[]{:S(2)}, u32[]{:S(2)}) collective-permute-start(f32[2,16,256]{2,1,0:T(8,128)S(1)} %get-tuple-element.240), channel_id=1, source_target_pairs={{0,1},{1,2},{2,3},{3,4},{4,5},{5,6},{6,7},{8,9},{9,10},{10,11},{11... | collective-permute-start | bytes 98312 | tf_op jit(solution)/shard_map/ppermute | solution.py:21
  45.5 2.5 collective-permute-done.9.refs_4_
  48.1 3.6 %collective-permute-start.10 = (f32[2,16,256]{2,1,0:T(8,128)S(1)}, f32[2,16,256]{2,1,0:T(8,128)S(1)}, u32[]{:S(2)}, u32[]{:S(2)}) collective-permute-start(f32[2,16,256]{2,1,0:T(8,128)S(1)} %get-tuple-element.252), channel_id=1, source_target_pairs={{0,8},{8,16},{16,24},{1,9},{9,17},{17,25},{2,10},{10,18},{18,26},{... | collective-permute-start | bytes 98312 | tf_op jit(solution)/shard_map/ppermute | solution.py:21
  51.7 4.5 %collective-permute-start.11 = (f32[2,16,256]{2,1,0:T(8,128)S(1)}, f32[2,16,256]{2,1,0:T(8,128)S(1)}, u32[]{:S(2)}, u32[]{:S(2)}) collective-permute-start(f32[2,16,256]{2,1,0:T(8,128)S(1)} %get-tuple-element.253), channel_id=1, source_target_pairs={{0,1},{1,2},{2,3},{3,4},{4,5},{5,6},{6,7},{8,9},{9,10},{10,11},{11... | collective-permute-start | bytes 98312 | tf_op jit(solution)/shard_map/ppermute | solution.py:21
  63.3 2.1 collective-permute-done.13.refs_4_
  65.4 3.8 %collective-permute-start.14 = (f32[2,16,256]{2,1,0:T(8,128)S(1)}, f32[2,16,256]{2,1,0:T(8,128)S(1)}, u32[]{:S(2)}, u32[]{:S(2)}) collective-permute-start(f32[2,16,256]{2,1,0:T(8,128)S(1)} %get-tuple-element.265), channel_id=1, source_target_pairs={{0,8},{8,16},{16,24},{1,9},{9,17},{17,25},{2,10},{10,18},{18,26},{... | collective-permute-start | bytes 98312 | tf_op jit(solution)/shard_map/ppermute | solution.py:21
  69.3 4.1 %collective-permute-start.15 = (f32[2,16,256]{2,1,0:T(8,128)S(1)}, f32[2,16,256]{2,1,0:T(8,128)S(1)}, u32[]{:S(2)}, u32[]{:S(2)}) collective-permute-start(f32[2,16,256]{2,1,0:T(8,128)S(1)} %get-tuple-element.266), channel_id=1, source_target_pairs={{0,1},{1,2},{2,3},{3,4},{4,5},{5,6},{6,7},{8,9},{9,10},{10,11},{11... | collective-permute-start | bytes 98312 | tf_op jit(solution)/shard_map/ppermute | solution.py:21
  80.4 2.1 collective-permute-done.17.refs_4_
  82.6 3.8 %collective-permute-start.18 = (f32[2,16,256]{2,1,0:T(8,128)S(1)}, f32[2,16,256]{2,1,0:T(8,128)S(1)}, u32[]{:S(2)}, u32[]{:S(2)}) collective-permute-start(f32[2,16,256]{2,1,0:T(8,128)S(1)} %get-tuple-element.278), channel_id=1, source_target_pairs={{0,8},{8,16},{16,24},{1,9},{9,17},{17,25},{2,10},{10,18},{18,26},{... | collective-permute-start | bytes 98312 | tf_op jit(solution)/shard_map/ppermute | solution.py:21
  86.4 4.1 %collective-permute-start.19 = (f32[2,16,256]{2,1,0:T(8,128)S(1)}, f32[2,16,256]{2,1,0:T(8,128)S(1)}, u32[]{:S(2)}, u32[]{:S(2)}) collective-permute-start(f32[2,16,256]{2,1,0:T(8,128)S(1)} %get-tuple-element.279), channel_id=1, source_target_pairs={{0,1},{1,2},{2,3},{3,4},{4,5},{5,6},{6,7},{8,9},{9,10},{10,11},{11... | collective-permute-start | bytes 98312 | tf_op jit(solution)/shard_map/ppermute | solution.py:21
  97.6 2.1 collective-permute-done.21.refs_4_
  99.8 3.8 %collective-permute-start.22 = (f32[2,16,256]{2,1,0:T(8,128)S(1)}, f32[2,16,256]{2,1,0:T(8,128)S(1)}, u32[]{:S(2)}, u32[]{:S(2)}) collective-permute-start(f32[2,16,256]{2,1,0:T(8,128)S(1)} %get-tuple-element.291), channel_id=1, source_target_pairs={{0,8},{8,16},{16,24},{1,9},{9,17},{17,25},{2,10},{10,18},{18,26},{... | collective-permute-start | bytes 98312 | tf_op jit(solution)/shard_map/ppermute | solution.py:21
  103.6 4.1 %collective-permute-start.23 = (f32[2,16,256]{2,1,0:T(8,128)S(1)}, f32[2,16,256]{2,1,0:T(8,128)S(1)}, u32[]{:S(2)}, u32[]{:S(2)}) collective-permute-start(f32[2,16,256]{2,1,0:T(8,128)S(1)} %get-tuple-element.292), channel_id=1, source_target_pairs={{0,1},{1,2},{2,3},{3,4},{4,5},{5,6},{6,7},{8,9},{9,10},{10,11},{11... | collective-permute-start | bytes 98312 | tf_op jit(solution)/shard_map/ppermute | solution.py:21
  114.8 2.1 collective-permute-done.25.refs_4_
  117.0 3.8 %collective-permute-start.26 = (f32[2,16,256]{2,1,0:T(8,128)S(1)}, f32[2,16,256]{2,1,0:T(8,128)S(1)}, u32[]{:S(2)}, u32[]{:S(2)}) collective-permute-start(f32[2,16,256]{2,1,0:T(8,128)S(1)} %get-tuple-element.304), channel_id=1, source_target_pairs={{0,8},{8,16},{16,24},{1,9},{9,17},{17,25},{2,10},{10,18},{18,26},{... | collective-permute-start | bytes 98312 | tf_op jit(solution)/shard_map/ppermute | solution.py:21
  120.8 4.1 %collective-permute-start.27 = (f32[2,16,256]{2,1,0:T(8,128)S(1)}, f32[2,16,256]{2,1,0:T(8,128)S(1)}, u32[]{:S(2)}, u32[]{:S(2)}) collective-permute-start(f32[2,16,256]{2,1,0:T(8,128)S(1)} %get-tuple-element.305), channel_id=1, source_target_pairs={{0,1},{1,2},{2,3},{3,4},{4,5},{5,6},{6,7},{8,9},{9,10},{10,11},{11... | collective-permute-start | bytes 98312 | tf_op jit(solution)/shard_map/ppermute | solution.py:21
  132.0 2.1 collective-permute-done.29.refs_4_
  134.1 3.8 %collective-permute-start.30 = (f32[2,16,256]{2,1,0:T(8,128)S(1)}, f32[2,16,256]{2,1,0:T(8,128)S(1)}, u32[]{:S(2)}, u32[]{:S(2)}) collective-permute-start(f32[2,16,256]{2,1,0:T(8,128)S(1)} %get-tuple-element.317), channel_id=1, source_target_pairs={{0,8},{8,16},{16,24},{1,9},{9,17},{17,25},{2,10},{10,18},{18,26},{... | collective-permute-start | bytes 98312 | tf_op jit(solution)/shard_map/ppermute | solution.py:21
  138.0 4.1 %collective-permute-start.31 = (f32[2,16,256]{2,1,0:T(8,128)S(1)}, f32[2,16,256]{2,1,0:T(8,128)S(1)}, u32[]{:S(2)}, u32[]{:S(2)}) collective-permute-start(f32[2,16,256]{2,1,0:T(8,128)S(1)} %get-tuple-element.318), channel_id=1, source_target_pairs={{0,1},{1,2},{2,3},{3,4},{4,5},{5,6},{6,7},{8,9},{9,10},{10,11},{11... | collective-permute-start | bytes 98312 | tf_op jit(solution)/shard_map/ppermute | solution.py:21
  149.1 2.1 collective-permute-done.33.refs_4_
  151.3 3.8 %collective-permute-start.34 = (f32[2,16,256]{2,1,0:T(8,128)S(1)}, f32[2,16,256]{2,1,0:T(8,128)S(1)}, u32[]{:S(2)}, u32[]{:S(2)}) collective-permute-start(f32[2,16,256]{2,1,0:T(8,128)S(1)} %get-tuple-element.330), channel_id=1, source_target_pairs={{0,8},{8,16},{16,24},{1,9},{9,17},{17,25},{2,10},{10,18},{18,26},{... | collective-permute-start | bytes 98312 | tf_op jit(solution)/shard_map/ppermute | solution.py:21
  155.1 4.1 %collective-permute-start.35 = (f32[2,16,256]{2,1,0:T(8,128)S(1)}, f32[2,16,256]{2,1,0:T(8,128)S(1)}, u32[]{:S(2)}, u32[]{:S(2)}) collective-permute-start(f32[2,16,256]{2,1,0:T(8,128)S(1)} %get-tuple-element.331), channel_id=1, source_target_pairs={{0,1},{1,2},{2,3},{3,4},{4,5},{5,6},{6,7},{8,9},{9,10},{10,11},{11... | collective-permute-start | bytes 98312 | tf_op jit(solution)/shard_map/ppermute | solution.py:21
  168.5 3.8 %collective-permute-start.38 = (f32[2,16,256]{2,1,0:T(8,128)S(1)}, f32[2,16,256]{2,1,0:T(8,128)S(1)}, u32[]{:S(2)}, u32[]{:S(2)}) collective-permute-start(f32[2,16,256]{2,1,0:T(8,128)S(1)} %get-tuple-element.343), channel_id=1, source_target_pairs={{0,8},{8,16},{16,24},{1,9},{9,17},{17,25},{2,10},{10,18},{18,26},{... | collective-permute-start | bytes 98312 | tf_op jit(solution)/shard_map/ppermute | solution.py:21
  172.3 4.3 %collective-permute-start.39 = (f32[2,16,256]{2,1,0:T(8,128)S(1)}, f32[2,16,256]{2,1,0:T(8,128)S(1)}, u32[]{:S(2)}, u32[]{:S(2)}) collective-permute-start(f32[2,16,256]{2,1,0:T(8,128)S(1)} %get-tuple-element.344), channel_id=1, source_target_pairs={{0,1},{1,2},{2,3},{3,4},{4,5},{5,6},{6,7},{8,9},{9,10},{10,11},{11... | collective-permute-start | bytes 98312 | tf_op jit(solution)/shard_map/ppermute | solution.py:21
  185.7 4.0 %collective-permute-start.42 = (f32[2,16,256]{2,1,0:T(8,128)S(1)}, f32[2,16,256]{2,1,0:T(8,128)S(1)}, u32[]{:S(2)}, u32[]{:S(2)}) collective-permute-start(f32[2,16,256]{2,1,0:T(8,128)S(1)} %get-tuple-element.356), channel_id=1, source_target_pairs={{0,8},{8,16},{16,24},{1,9},{9,17},{17,25},{2,10},{10,18},{18,26},{... | collective-permute-start | bytes 98312 | tf_op jit(solution)/shard_map/ppermute | solution.py:21
  189.7 4.0 %collective-permute-start.43 = (f32[2,16,256]{2,1,0:T(8,128)S(1)}, f32[2,16,256]{2,1,0:T(8,128)S(1)}, u32[]{:S(2)}, u32[]{:S(2)}) collective-permute-start(f32[2,16,256]{2,1,0:T(8,128)S(1)} %get-tuple-element.357), channel_id=1, source_target_pairs={{0,1},{1,2},{2,3},{3,4},{4,5},{5,6},{6,7},{8,9},{9,10},{10,11},{11... | collective-permute-start | bytes 98312 | tf_op jit(solution)/shard_map/ppermute | solution.py:21
  200.7 2.1 collective-permute-done.45.refs_4_
  202.9 3.8 %collective-permute-start.46 = (f32[2,16,256]{2,1,0:T(8,128)S(1)}, f32[2,16,256]{2,1,0:T(8,128)S(1)}, u32[]{:S(2)}, u32[]{:S(2)}) collective-permute-start(f32[2,16,256]{2,1,0:T(8,128)S(1)} %get-tuple-element.369), channel_id=1, source_target_pairs={{0,8},{8,16},{16,24},{1,9},{9,17},{17,25},{2,10},{10,18},{18,26},{... | collective-permute-start | bytes 98312 | tf_op jit(solution)/shard_map/ppermute | solution.py:21
  206.7 4.1 %collective-permute-start.47 = (f32[2,16,256]{2,1,0:T(8,128)S(1)}, f32[2,16,256]{2,1,0:T(8,128)S(1)}, u32[]{:S(2)}, u32[]{:S(2)}) collective-permute-start(f32[2,16,256]{2,1,0:T(8,128)S(1)} %get-tuple-element.370), channel_id=1, source_target_pairs={{0,1},{1,2},{2,3},{3,4},{4,5},{5,6},{6,7},{8,9},{9,10},{10,11},{11... | collective-permute-start | bytes 98312 | tf_op jit(solution)/shard_map/ppermute | solution.py:21
  217.9 2.1 collective-permute-done.49.refs_4_
  220.1 3.8 %collective-permute-start.50 = (f32[2,16,256]{2,1,0:T(8,128)S(1)}, f32[2,16,256]{2,1,0:T(8,128)S(1)}, u32[]{:S(2)}, u32[]{:S(2)}) collective-permute-start(f32[2,16,256]{2,1,0:T(8,128)S(1)} %get-tuple-element.382), channel_id=1, source_target_pairs={{0,8},{8,16},{16,24},{1,9},{9,17},{17,25},{2,10},{10,18},{18,26},{... | collective-permute-start | bytes 98312 | tf_op jit(solution)/shard_map/ppermute | solution.py:21
  223.9 4.1 %collective-permute-start.51 = (f32[2,16,256]{2,1,0:T(8,128)S(1)}, f32[2,16,256]{2,1,0:T(8,128)S(1)}, u32[]{:S(2)}, u32[]{:S(2)}) collective-permute-start(f32[2,16,256]{2,1,0:T(8,128)S(1)} %get-tuple-element.383), channel_id=1, source_target_pairs={{0,1},{1,2},{2,3},{3,4},{4,5},{5,6},{6,7},{8,9},{9,10},{10,11},{11... | collective-permute-start | bytes 98312 | tf_op jit(solution)/shard_map/ppermute | solution.py:21
  237.2 3.8 %collective-permute-start.54 = (f32[2,16,256]{2,1,0:T(8,128)S(1)}, f32[2,16,256]{2,1,0:T(8,128)S(1)}, u32[]{:S(2)}, u32[]{:S(2)}) collective-permute-start(f32[2,16,256]{2,1,0:T(8,128)S(1)} %get-tuple-element.395), channel_id=1, source_target_pairs={{0,8},{8,16},{16,24},{1,9},{9,17},{17,25},{2,10},{10,18},{18,26},{... | collective-permute-start | bytes 98312 | tf_op jit(solution)/shard_map/ppermute | solution.py:21
  241.1 4.1 %collective-permute-start.55 = (f32[2,16,256]{2,1,0:T(8,128)S(1)}, f32[2,16,256]{2,1,0:T(8,128)S(1)}, u32[]{:S(2)}, u32[]{:S(2)}) collective-permute-start(f32[2,16,256]{2,1,0:T(8,128)S(1)} %get-tuple-element.396), channel_id=1, source_target_pairs={{0,1},{1,2},{2,3},{3,4},{4,5},{5,6},{6,7},{8,9},{9,10},{10,11},{11... | collective-permute-start | bytes 98312 | tf_op jit(solution)/shard_map/ppermute | solution.py:21
  254.4 3.8 %collective-permute-start.58 = (f32[2,16,256]{2,1,0:T(8,128)S(1)}, f32[2,16,256]{2,1,0:T(8,128)S(1)}, u32[]{:S(2)}, u32[]{:S(2)}) collective-permute-start(f32[2,16,256]{2,1,0:T(8,128)S(1)} %get-tuple-element.408), channel_id=1, source_target_pairs={{0,8},{8,16},{16,24},{1,9},{9,17},{17,25},{2,10},{10,18},{18,26},{... | collective-permute-start | bytes 98312 | tf_op jit(solution)/shard_map/ppermute | solution.py:21
  258.2 4.1 %collective-permute-start.59 = (f32[2,16,256]{2,1,0:T(8,128)S(1)}, f32[2,16,256]{2,1,0:T(8,128)S(1)}, u32[]{:S(2)}, u32[]{:S(2)}) collective-permute-start(f32[2,16,256]{2,1,0:T(8,128)S(1)} %get-tuple-element.409), channel_id=1, source_target_pairs={{0,1},{1,2},{2,3},{3,4},{4,5},{5,6},{6,7},{8,9},{9,10},{10,11},{11... | collective-permute-start | bytes 98312 | tf_op jit(solution)/shard_map/ppermute | solution.py:21
  272.2 3.8 %collective-permute-start.62 = (f32[2,16,256]{2,1,0:T(8,128)}, f32[2,16,256]{2,1,0:T(8,128)S(1)}, u32[]{:S(2)}, u32[]{:S(2)}) collective-permute-start(f32[2,16,256]{2,1,0:T(8,128)} %get-tuple-element.421), channel_id=1, source_target_pairs={{0,8},{8,16},{16,24},{1,9},{9,17},{17,25},{2,10},{10,18},{18,26},{... | collective-permute-start | bytes 98312 | tf_op jit(solution)/shard_map/ppermute | solution.py:21
  276.1 4.1 %collective-permute-start.63 = (f32[2,16,256]{2,1,0:T(8,128)S(1)}, f32[2,16,256]{2,1,0:T(8,128)S(1)}, u32[]{:S(2)}, u32[]{:S(2)}) collective-permute-start(f32[2,16,256]{2,1,0:T(8,128)S(1)} %get-tuple-element.422), channel_id=1, source_target_pairs={{0,1},{1,2},{2,3},{3,4},{4,5},{5,6},{6,7},{8,9},{9,10},{10,11},{11... | collective-permute-start | bytes 98312 | tf_op jit(solution)/shard_map/ppermute | solution.py:21
  313.1 2.6 collective-permute-start.64
  317.1 3.4 %collective-permute-done.65 = f32[16,512]{1,0:T(8,128)S(1)} collective-permute-done((f32[16,512]{1,0:T(8,128)S(1)}, f32[16,512]{1,0:T(8,128)S(1)}, u32[]{:S(2)}, u32[]{:S(2)}) %collective-permute-start.65) | collective-permute-done | bytes 32800 | tf_op jit(solution)/shard_map/ppermute | solution.py:188
  321.6 2.8 collective-permute-done.66
  326.0 2.3 collective-permute-done.67
  328.3 2.7 collective-permute-start.68
  (315 shorter events, 163.2 us)
Async XLA Ops:
  5.4 7.3 %collective-permute-start.1 = (f32[2,16,256]{2,1,0:T(8,128)S(1)}, f32[2,16,256]{2,1,0:T(8,128)S(1)}, u32[]{:S(2)}, u32[]{:S(2)}) collective-permute-start(f32[2,16,256]{2,1,0:T(8,128)S(1)} %pad_maximum_fusion.1), channel_id=1, source_target_pairs={{1,0},{2,1},{3,2},{4,3},{5,4},{6,5},{7,6},{9,8},{10,9},{11,10},{12... | collective-permute-start | bytes 98312 | tf_op jit(solution)/shard_map/ppermute | solution.py:21
  6.8 5.9 %collective-permute-start = (f32[2,16,256]{2,1,0:T(8,128)S(1)}, f32[2,16,256]{2,1,0:T(8,128)S(1)}, u32[]{:S(2)}, u32[]{:S(2)}) collective-permute-start(f32[2,16,256]{2,1,0:T(8,128)S(1)} %pad_maximum_fusion), channel_id=1, source_target_pairs={{8,0},{16,8},{24,16},{9,1},{17,9},{25,17},{10,2},{18,10},{26,18},{... | collective-permute-start | bytes 98312 | tf_op jit(solution)/shard_map/ppermute | solution.py:21
  12.8 10.2 %collective-permute-start.2 = (f32[2,16,256]{2,1,0:T(8,128)S(1)}, f32[2,16,256]{2,1,0:T(8,128)S(1)}, u32[]{:S(2)}, u32[]{:S(2)}) collective-permute-start(f32[2,16,256]{2,1,0:T(8,128)S(1)} %get-tuple-element.226), channel_id=1, source_target_pairs={{0,8},{8,16},{16,24},{1,9},{9,17},{17,25},{2,10},{10,18},{18,26},{... | collective-permute-start | bytes 98312 | tf_op jit(solution)/shard_map/ppermute | solution.py:21
  16.0 7.1 %collective-permute-start.3 = (f32[2,16,256]{2,1,0:T(8,128)S(1)}, f32[2,16,256]{2,1,0:T(8,128)S(1)}, u32[]{:S(2)}, u32[]{:S(2)}) collective-permute-start(f32[2,16,256]{2,1,0:T(8,128)S(1)} %get-tuple-element.227), channel_id=1, source_target_pairs={{0,1},{1,2},{2,3},{3,4},{4,5},{5,6},{6,7},{8,9},{9,10},{10,11},{11... | collective-permute-start | bytes 98312 | tf_op jit(solution)/shard_map/ppermute | solution.py:21
  24.5 6.8 %collective-permute-start.5 = (f32[2,16,256]{2,1,0:T(8,128)S(1)}, f32[2,16,256]{2,1,0:T(8,128)S(1)}, u32[]{:S(2)}, u32[]{:S(2)}) collective-permute-start(f32[2,16,256]{2,1,0:T(8,128)S(1)} %get-tuple-element.233), channel_id=1, source_target_pairs={{1,0},{2,1},{3,2},{4,3},{5,4},{6,5},{7,6},{9,8},{10,9},{11,10},{12... | collective-permute-start | bytes 98312 | tf_op jit(solution)/shard_map/ppermute | solution.py:21
  31.4 9.3 %collective-permute-start.6 = (f32[2,16,256]{2,1,0:T(8,128)S(1)}, f32[2,16,256]{2,1,0:T(8,128)S(1)}, u32[]{:S(2)}, u32[]{:S(2)}) collective-permute-start(f32[2,16,256]{2,1,0:T(8,128)S(1)} %get-tuple-element.239), channel_id=1, source_target_pairs={{0,8},{8,16},{16,24},{1,9},{9,17},{17,25},{2,10},{10,18},{18,26},{... | collective-permute-start | bytes 98312 | tf_op jit(solution)/shard_map/ppermute | solution.py:21
  33.8 6.9 %collective-permute-start.7 = (f32[2,16,256]{2,1,0:T(8,128)S(1)}, f32[2,16,256]{2,1,0:T(8,128)S(1)}, u32[]{:S(2)}, u32[]{:S(2)}) collective-permute-start(f32[2,16,256]{2,1,0:T(8,128)S(1)} %get-tuple-element.240), channel_id=1, source_target_pairs={{0,1},{1,2},{2,3},{3,4},{4,5},{5,6},{6,7},{8,9},{9,10},{10,11},{11... | collective-permute-start | bytes 98312 | tf_op jit(solution)/shard_map/ppermute | solution.py:21
  42.1 5.9 %collective-permute-start.9 = (f32[2,16,256]{2,1,0:T(8,128)S(1)}, f32[2,16,256]{2,1,0:T(8,128)S(1)}, u32[]{:S(2)}, u32[]{:S(2)}) collective-permute-start(f32[2,16,256]{2,1,0:T(8,128)S(1)} %get-tuple-element.246), channel_id=1, source_target_pairs={{1,0},{2,1},{3,2},{4,3},{5,4},{6,5},{7,6},{9,8},{10,9},{11,10},{12... | collective-permute-start | bytes 98312 | tf_op jit(solution)/shard_map/ppermute | solution.py:21
  48.1 9.8 %collective-permute-start.10 = (f32[2,16,256]{2,1,0:T(8,128)S(1)}, f32[2,16,256]{2,1,0:T(8,128)S(1)}, u32[]{:S(2)}, u32[]{:S(2)}) collective-permute-start(f32[2,16,256]{2,1,0:T(8,128)S(1)} %get-tuple-element.252), channel_id=1, source_target_pairs={{0,8},{8,16},{16,24},{1,9},{9,17},{17,25},{2,10},{10,18},{18,26},{... | collective-permute-start | bytes 98312 | tf_op jit(solution)/shard_map/ppermute | solution.py:21
  51.7 6.2 %collective-permute-start.11 = (f32[2,16,256]{2,1,0:T(8,128)S(1)}, f32[2,16,256]{2,1,0:T(8,128)S(1)}, u32[]{:S(2)}, u32[]{:S(2)}) collective-permute-start(f32[2,16,256]{2,1,0:T(8,128)S(1)} %get-tuple-element.253), channel_id=1, source_target_pairs={{0,1},{1,2},{2,3},{3,4},{4,5},{5,6},{6,7},{8,9},{9,10},{10,11},{11... | collective-permute-start | bytes 98312 | tf_op jit(solution)/shard_map/ppermute | solution.py:21
  59.3 6.0 %collective-permute-start.13 = (f32[2,16,256]{2,1,0:T(8,128)S(1)}, f32[2,16,256]{2,1,0:T(8,128)S(1)}, u32[]{:S(2)}, u32[]{:S(2)}) collective-permute-start(f32[2,16,256]{2,1,0:T(8,128)S(1)} %get-tuple-element.259), channel_id=1, source_target_pairs={{1,0},{2,1},{3,2},{4,3},{5,4},{6,5},{7,6},{9,8},{10,9},{11,10},{12... | collective-permute-start | bytes 98312 | tf_op jit(solution)/shard_map/ppermute | solution.py:21
  65.4 9.6 %collective-permute-start.14 = (f32[2,16,256]{2,1,0:T(8,128)S(1)}, f32[2,16,256]{2,1,0:T(8,128)S(1)}, u32[]{:S(2)}, u32[]{:S(2)}) collective-permute-start(f32[2,16,256]{2,1,0:T(8,128)S(1)} %get-tuple-element.265), channel_id=1, source_target_pairs={{0,8},{8,16},{16,24},{1,9},{9,17},{17,25},{2,10},{10,18},{18,26},{... | collective-permute-start | bytes 98312 | tf_op jit(solution)/shard_map/ppermute | solution.py:21
  69.3 5.8 %collective-permute-start.15 = (f32[2,16,256]{2,1,0:T(8,128)S(1)}, f32[2,16,256]{2,1,0:T(8,128)S(1)}, u32[]{:S(2)}, u32[]{:S(2)}) collective-permute-start(f32[2,16,256]{2,1,0:T(8,128)S(1)} %get-tuple-element.266), channel_id=1, source_target_pairs={{0,1},{1,2},{2,3},{3,4},{4,5},{5,6},{6,7},{8,9},{9,10},{10,11},{11... | collective-permute-start | bytes 98312 | tf_op jit(solution)/shard_map/ppermute | solution.py:21
  76.5 6.0 %collective-permute-start.17 = (f32[2,16,256]{2,1,0:T(8,128)S(1)}, f32[2,16,256]{2,1,0:T(8,128)S(1)}, u32[]{:S(2)}, u32[]{:S(2)}) collective-permute-start(f32[2,16,256]{2,1,0:T(8,128)S(1)} %get-tuple-element.272), channel_id=1, source_target_pairs={{1,0},{2,1},{3,2},{4,3},{5,4},{6,5},{7,6},{9,8},{10,9},{11,10},{12... | collective-permute-start | bytes 98312 | tf_op jit(solution)/shard_map/ppermute | solution.py:21
  82.6 9.6 %collective-permute-start.18 = (f32[2,16,256]{2,1,0:T(8,128)S(1)}, f32[2,16,256]{2,1,0:T(8,128)S(1)}, u32[]{:S(2)}, u32[]{:S(2)}) collective-permute-start(f32[2,16,256]{2,1,0:T(8,128)S(1)} %get-tuple-element.278), channel_id=1, source_target_pairs={{0,8},{8,16},{16,24},{1,9},{9,17},{17,25},{2,10},{10,18},{18,26},{... | collective-permute-start | bytes 98312 | tf_op jit(solution)/shard_map/ppermute | solution.py:21
  86.4 5.8 %collective-permute-start.19 = (f32[2,16,256]{2,1,0:T(8,128)S(1)}, f32[2,16,256]{2,1,0:T(8,128)S(1)}, u32[]{:S(2)}, u32[]{:S(2)}) collective-permute-start(f32[2,16,256]{2,1,0:T(8,128)S(1)} %get-tuple-element.279), channel_id=1, source_target_pairs={{0,1},{1,2},{2,3},{3,4},{4,5},{5,6},{6,7},{8,9},{9,10},{10,11},{11... | collective-permute-start | bytes 98312 | tf_op jit(solution)/shard_map/ppermute | solution.py:21
  93.7 6.0 %collective-permute-start.21 = (f32[2,16,256]{2,1,0:T(8,128)S(1)}, f32[2,16,256]{2,1,0:T(8,128)S(1)}, u32[]{:S(2)}, u32[]{:S(2)}) collective-permute-start(f32[2,16,256]{2,1,0:T(8,128)S(1)} %get-tuple-element.285), channel_id=1, source_target_pairs={{1,0},{2,1},{3,2},{4,3},{5,4},{6,5},{7,6},{9,8},{10,9},{11,10},{12... | collective-permute-start | bytes 98312 | tf_op jit(solution)/shard_map/ppermute | solution.py:21
  99.8 9.7 %collective-permute-start.22 = (f32[2,16,256]{2,1,0:T(8,128)S(1)}, f32[2,16,256]{2,1,0:T(8,128)S(1)}, u32[]{:S(2)}, u32[]{:S(2)}) collective-permute-start(f32[2,16,256]{2,1,0:T(8,128)S(1)} %get-tuple-element.291), channel_id=1, source_target_pairs={{0,8},{8,16},{16,24},{1,9},{9,17},{17,25},{2,10},{10,18},{18,26},{... | collective-permute-start | bytes 98312 | tf_op jit(solution)/shard_map/ppermute | solution.py:21
  103.6 5.8 %collective-permute-start.23 = (f32[2,16,256]{2,1,0:T(8,128)S(1)}, f32[2,16,256]{2,1,0:T(8,128)S(1)}, u32[]{:S(2)}, u32[]{:S(2)}) collective-permute-start(f32[2,16,256]{2,1,0:T(8,128)S(1)} %get-tuple-element.292), channel_id=1, source_target_pairs={{0,1},{1,2},{2,3},{3,4},{4,5},{5,6},{6,7},{8,9},{9,10},{10,11},{11... | collective-permute-start | bytes 98312 | tf_op jit(solution)/shard_map/ppermute | solution.py:21
  110.9 6.0 %collective-permute-start.25 = (f32[2,16,256]{2,1,0:T(8,128)S(1)}, f32[2,16,256]{2,1,0:T(8,128)S(1)}, u32[]{:S(2)}, u32[]{:S(2)}) collective-permute-start(f32[2,16,256]{2,1,0:T(8,128)S(1)} %get-tuple-element.298), channel_id=1, source_target_pairs={{1,0},{2,1},{3,2},{4,3},{5,4},{6,5},{7,6},{9,8},{10,9},{11,10},{12... | collective-permute-start | bytes 98312 | tf_op jit(solution)/shard_map/ppermute | solution.py:21
  117.0 9.6 %collective-permute-start.26 = (f32[2,16,256]{2,1,0:T(8,128)S(1)}, f32[2,16,256]{2,1,0:T(8,128)S(1)}, u32[]{:S(2)}, u32[]{:S(2)}) collective-permute-start(f32[2,16,256]{2,1,0:T(8,128)S(1)} %get-tuple-element.304), channel_id=1, source_target_pairs={{0,8},{8,16},{16,24},{1,9},{9,17},{17,25},{2,10},{10,18},{18,26},{... | collective-permute-start | bytes 98312 | tf_op jit(solution)/shard_map/ppermute | solution.py:21
  120.8 5.8 %collective-permute-start.27 = (f32[2,16,256]{2,1,0:T(8,128)S(1)}, f32[2,16,256]{2,1,0:T(8,128)S(1)}, u32[]{:S(2)}, u32[]{:S(2)}) collective-permute-start(f32[2,16,256]{2,1,0:T(8,128)S(1)} %get-tuple-element.305), channel_id=1, source_target_pairs={{0,1},{1,2},{2,3},{3,4},{4,5},{5,6},{6,7},{8,9},{9,10},{10,11},{11... | collective-permute-start | bytes 98312 | tf_op jit(solution)/shard_map/ppermute | solution.py:21
  128.0 6.0 %collective-permute-start.29 = (f32[2,16,256]{2,1,0:T(8,128)S(1)}, f32[2,16,256]{2,1,0:T(8,128)S(1)}, u32[]{:S(2)}, u32[]{:S(2)}) collective-permute-start(f32[2,16,256]{2,1,0:T(8,128)S(1)} %get-tuple-element.311), channel_id=1, source_target_pairs={{1,0},{2,1},{3,2},{4,3},{5,4},{6,5},{7,6},{9,8},{10,9},{11,10},{12... | collective-permute-start | bytes 98312 | tf_op jit(solution)/shard_map/ppermute | solution.py:21
  134.1 9.7 %collective-permute-start.30 = (f32[2,16,256]{2,1,0:T(8,128)S(1)}, f32[2,16,256]{2,1,0:T(8,128)S(1)}, u32[]{:S(2)}, u32[]{:S(2)}) collective-permute-start(f32[2,16,256]{2,1,0:T(8,128)S(1)} %get-tuple-element.317), channel_id=1, source_target_pairs={{0,8},{8,16},{16,24},{1,9},{9,17},{17,25},{2,10},{10,18},{18,26},{... | collective-permute-start | bytes 98312 | tf_op jit(solution)/shard_map/ppermute | solution.py:21
  138.0 5.8 %collective-permute-start.31 = (f32[2,16,256]{2,1,0:T(8,128)S(1)}, f32[2,16,256]{2,1,0:T(8,128)S(1)}, u32[]{:S(2)}, u32[]{:S(2)}) collective-permute-start(f32[2,16,256]{2,1,0:T(8,128)S(1)} %get-tuple-element.318), channel_id=1, source_target_pairs={{0,1},{1,2},{2,3},{3,4},{4,5},{5,6},{6,7},{8,9},{9,10},{10,11},{11... | collective-permute-start | bytes 98312 | tf_op jit(solution)/shard_map/ppermute | solution.py:21
  145.2 6.0 %collective-permute-start.33 = (f32[2,16,256]{2,1,0:T(8,128)S(1)}, f32[2,16,256]{2,1,0:T(8,128)S(1)}, u32[]{:S(2)}, u32[]{:S(2)}) collective-permute-start(f32[2,16,256]{2,1,0:T(8,128)S(1)} %get-tuple-element.324), channel_id=1, source_target_pairs={{1,0},{2,1},{3,2},{4,3},{5,4},{6,5},{7,6},{9,8},{10,9},{11,10},{12... | collective-permute-start | bytes 98312 | tf_op jit(solution)/shard_map/ppermute | solution.py:21
  151.3 9.7 %collective-permute-start.34 = (f32[2,16,256]{2,1,0:T(8,128)S(1)}, f32[2,16,256]{2,1,0:T(8,128)S(1)}, u32[]{:S(2)}, u32[]{:S(2)}) collective-permute-start(f32[2,16,256]{2,1,0:T(8,128)S(1)} %get-tuple-element.330), channel_id=1, source_target_pairs={{0,8},{8,16},{16,24},{1,9},{9,17},{17,25},{2,10},{10,18},{18,26},{... | collective-permute-start | bytes 98312 | tf_op jit(solution)/shard_map/ppermute | solution.py:21
  155.1 5.8 %collective-permute-start.35 = (f32[2,16,256]{2,1,0:T(8,128)S(1)}, f32[2,16,256]{2,1,0:T(8,128)S(1)}, u32[]{:S(2)}, u32[]{:S(2)}) collective-permute-start(f32[2,16,256]{2,1,0:T(8,128)S(1)} %get-tuple-element.331), channel_id=1, source_target_pairs={{0,1},{1,2},{2,3},{3,4},{4,5},{5,6},{6,7},{8,9},{9,10},{10,11},{11... | collective-permute-start | bytes 98312 | tf_op jit(solution)/shard_map/ppermute | solution.py:21
  162.4 6.0 %collective-permute-start.37 = (f32[2,16,256]{2,1,0:T(8,128)S(1)}, f32[2,16,256]{2,1,0:T(8,128)S(1)}, u32[]{:S(2)}, u32[]{:S(2)}) collective-permute-start(f32[2,16,256]{2,1,0:T(8,128)S(1)} %get-tuple-element.337), channel_id=1, source_target_pairs={{1,0},{2,1},{3,2},{4,3},{5,4},{6,5},{7,6},{9,8},{10,9},{11,10},{12... | collective-permute-start | bytes 98312 | tf_op jit(solution)/shard_map/ppermute | solution.py:21
  168.5 9.8 %collective-permute-start.38 = (f32[2,16,256]{2,1,0:T(8,128)S(1)}, f32[2,16,256]{2,1,0:T(8,128)S(1)}, u32[]{:S(2)}, u32[]{:S(2)}) collective-permute-start(f32[2,16,256]{2,1,0:T(8,128)S(1)} %get-tuple-element.343), channel_id=1, source_target_pairs={{0,8},{8,16},{16,24},{1,9},{9,17},{17,25},{2,10},{10,18},{18,26},{... | collective-permute-start | bytes 98312 | tf_op jit(solution)/shard_map/ppermute | solution.py:21
  172.3 6.0 %collective-permute-start.39 = (f32[2,16,256]{2,1,0:T(8,128)S(1)}, f32[2,16,256]{2,1,0:T(8,128)S(1)}, u32[]{:S(2)}, u32[]{:S(2)}) collective-permute-start(f32[2,16,256]{2,1,0:T(8,128)S(1)} %get-tuple-element.344), channel_id=1, source_target_pairs={{0,1},{1,2},{2,3},{3,4},{4,5},{5,6},{6,7},{8,9},{9,10},{10,11},{11... | collective-permute-start | bytes 98312 | tf_op jit(solution)/shard_map/ppermute | solution.py:21
  179.8 5.8 %collective-permute-start.41 = (f32[2,16,256]{2,1,0:T(8,128)S(1)}, f32[2,16,256]{2,1,0:T(8,128)S(1)}, u32[]{:S(2)}, u32[]{:S(2)}) collective-permute-start(f32[2,16,256]{2,1,0:T(8,128)S(1)} %get-tuple-element.350), channel_id=1, source_target_pairs={{1,0},{2,1},{3,2},{4,3},{5,4},{6,5},{7,6},{9,8},{10,9},{11,10},{12... | collective-permute-start | bytes 98312 | tf_op jit(solution)/shard_map/ppermute | solution.py:21
  185.7 9.7 %collective-permute-start.42 = (f32[2,16,256]{2,1,0:T(8,128)S(1)}, f32[2,16,256]{2,1,0:T(8,128)S(1)}, u32[]{:S(2)}, u32[]{:S(2)}) collective-permute-start(f32[2,16,256]{2,1,0:T(8,128)S(1)} %get-tuple-element.356), channel_id=1, source_target_pairs={{0,8},{8,16},{16,24},{1,9},{9,17},{17,25},{2,10},{10,18},{18,26},{... | collective-permute-start | bytes 98312 | tf_op jit(solution)/shard_map/ppermute | solution.py:21
  196.8 6.0 %collective-permute-start.45 = (f32[2,16,256]{2,1,0:T(8,128)S(1)}, f32[2,16,256]{2,1,0:T(8,128)S(1)}, u32[]{:S(2)}, u32[]{:S(2)}) collective-permute-start(f32[2,16,256]{2,1,0:T(8,128)S(1)} %get-tuple-element.363), channel_id=1, source_target_pairs={{1,0},{2,1},{3,2},{4,3},{5,4},{6,5},{7,6},{9,8},{10,9},{11,10},{12... | collective-permute-start | bytes 98312 | tf_op jit(solution)/shard_map/ppermute | solution.py:21
  202.9 9.6 %collective-permute-start.46 = (f32[2,16,256]{2,1,0:T(8,128)S(1)}, f32[2,16,256]{2,1,0:T(8,128)S(1)}, u32[]{:S(2)}, u32[]{:S(2)}) collective-permute-start(f32[2,16,256]{2,1,0:T(8,128)S(1)} %get-tuple-element.369), channel_id=1, source_target_pairs={{0,8},{8,16},{16,24},{1,9},{9,17},{17,25},{2,10},{10,18},{18,26},{... | collective-permute-start | bytes 98312 | tf_op jit(solution)/shard_map/ppermute | solution.py:21
  206.7 5.8 %collective-permute-start.47 = (f32[2,16,256]{2,1,0:T(8,128)S(1)}, f32[2,16,256]{2,1,0:T(8,128)S(1)}, u32[]{:S(2)}, u32[]{:S(2)}) collective-permute-start(f32[2,16,256]{2,1,0:T(8,128)S(1)} %get-tuple-element.370), channel_id=1, source_target_pairs={{0,1},{1,2},{2,3},{3,4},{4,5},{5,6},{6,7},{8,9},{9,10},{10,11},{11... | collective-permute-start | bytes 98312 | tf_op jit(solution)/shard_map/ppermute | solution.py:21
  214.0 6.0 %collective-permute-start.49 = (f32[2,16,256]{2,1,0:T(8,128)S(1)}, f32[2,16,256]{2,1,0:T(8,128)S(1)}, u32[]{:S(2)}, u32[]{:S(2)}) collective-permute-start(f32[2,16,256]{2,1,0:T(8,128)S(1)} %get-tuple-element.376), channel_id=1, source_target_pairs={{1,0},{2,1},{3,2},{4,3},{5,4},{6,5},{7,6},{9,8},{10,9},{11,10},{12... | collective-permute-start | bytes 98312 | tf_op jit(solution)/shard_map/ppermute | solution.py:21
  220.1 9.7 %collective-permute-start.50 = (f32[2,16,256]{2,1,0:T(8,128)S(1)}, f32[2,16,256]{2,1,0:T(8,128)S(1)}, u32[]{:S(2)}, u32[]{:S(2)}) collective-permute-start(f32[2,16,256]{2,1,0:T(8,128)S(1)} %get-tuple-element.382), channel_id=1, source_target_pairs={{0,8},{8,16},{16,24},{1,9},{9,17},{17,25},{2,10},{10,18},{18,26},{... | collective-permute-start | bytes 98312 | tf_op jit(solution)/shard_map/ppermute | solution.py:21
  223.9 5.8 %collective-permute-start.51 = (f32[2,16,256]{2,1,0:T(8,128)S(1)}, f32[2,16,256]{2,1,0:T(8,128)S(1)}, u32[]{:S(2)}, u32[]{:S(2)}) collective-permute-start(f32[2,16,256]{2,1,0:T(8,128)S(1)} %get-tuple-element.383), channel_id=1, source_target_pairs={{0,1},{1,2},{2,3},{3,4},{4,5},{5,6},{6,7},{8,9},{9,10},{10,11},{11... | collective-permute-start | bytes 98312 | tf_op jit(solution)/shard_map/ppermute | solution.py:21
  231.2 6.0 %collective-permute-start.53 = (f32[2,16,256]{2,1,0:T(8,128)S(1)}, f32[2,16,256]{2,1,0:T(8,128)S(1)}, u32[]{:S(2)}, u32[]{:S(2)}) collective-permute-start(f32[2,16,256]{2,1,0:T(8,128)S(1)} %get-tuple-element.389), channel_id=1, source_target_pairs={{1,0},{2,1},{3,2},{4,3},{5,4},{6,5},{7,6},{9,8},{10,9},{11,10},{12... | collective-permute-start | bytes 98312 | tf_op jit(solution)/shard_map/ppermute | solution.py:21
  237.2 9.6 %collective-permute-start.54 = (f32[2,16,256]{2,1,0:T(8,128)S(1)}, f32[2,16,256]{2,1,0:T(8,128)S(1)}, u32[]{:S(2)}, u32[]{:S(2)}) collective-permute-start(f32[2,16,256]{2,1,0:T(8,128)S(1)} %get-tuple-element.395), channel_id=1, source_target_pairs={{0,8},{8,16},{16,24},{1,9},{9,17},{17,25},{2,10},{10,18},{18,26},{... | collective-permute-start | bytes 98312 | tf_op jit(solution)/shard_map/ppermute | solution.py:21
  241.1 5.8 %collective-permute-start.55 = (f32[2,16,256]{2,1,0:T(8,128)S(1)}, f32[2,16,256]{2,1,0:T(8,128)S(1)}, u32[]{:S(2)}, u32[]{:S(2)}) collective-permute-start(f32[2,16,256]{2,1,0:T(8,128)S(1)} %get-tuple-element.396), channel_id=1, source_target_pairs={{0,1},{1,2},{2,3},{3,4},{4,5},{5,6},{6,7},{8,9},{9,10},{10,11},{11... | collective-permute-start | bytes 98312 | tf_op jit(solution)/shard_map/ppermute | solution.py:21
  248.3 6.0 %collective-permute-start.57 = (f32[2,16,256]{2,1,0:T(8,128)S(1)}, f32[2,16,256]{2,1,0:T(8,128)S(1)}, u32[]{:S(2)}, u32[]{:S(2)}) collective-permute-start(f32[2,16,256]{2,1,0:T(8,128)S(1)} %get-tuple-element.402), channel_id=1, source_target_pairs={{1,0},{2,1},{3,2},{4,3},{5,4},{6,5},{7,6},{9,8},{10,9},{11,10},{12... | collective-permute-start | bytes 98312 | tf_op jit(solution)/shard_map/ppermute | solution.py:21
  254.4 9.7 %collective-permute-start.58 = (f32[2,16,256]{2,1,0:T(8,128)S(1)}, f32[2,16,256]{2,1,0:T(8,128)S(1)}, u32[]{:S(2)}, u32[]{:S(2)}) collective-permute-start(f32[2,16,256]{2,1,0:T(8,128)S(1)} %get-tuple-element.408), channel_id=1, source_target_pairs={{0,8},{8,16},{16,24},{1,9},{9,17},{17,25},{2,10},{10,18},{18,26},{... | collective-permute-start | bytes 98312 | tf_op jit(solution)/shard_map/ppermute | solution.py:21
  258.2 5.8 %collective-permute-start.59 = (f32[2,16,256]{2,1,0:T(8,128)S(1)}, f32[2,16,256]{2,1,0:T(8,128)S(1)}, u32[]{:S(2)}, u32[]{:S(2)}) collective-permute-start(f32[2,16,256]{2,1,0:T(8,128)S(1)} %get-tuple-element.409), channel_id=1, source_target_pairs={{0,1},{1,2},{2,3},{3,4},{4,5},{5,6},{6,7},{8,9},{9,10},{10,11},{11... | collective-permute-start | bytes 98312 | tf_op jit(solution)/shard_map/ppermute | solution.py:21
  265.5 5.9 %collective-permute-start.61 = (f32[2,16,256]{2,1,0:T(8,128)S(1)}, f32[2,16,256]{2,1,0:T(8,128)S(1)}, u32[]{:S(2)}, u32[]{:S(2)}) collective-permute-start(f32[2,16,256]{2,1,0:T(8,128)S(1)} %get-tuple-element.415), channel_id=1, source_target_pairs={{1,0},{2,1},{3,2},{4,3},{5,4},{6,5},{7,6},{9,8},{10,9},{11,10},{12... | collective-permute-start | bytes 98312 | tf_op jit(solution)/shard_map/ppermute | solution.py:21
  272.2 38.7 %collective-permute-start.62 = (f32[2,16,256]{2,1,0:T(8,128)}, f32[2,16,256]{2,1,0:T(8,128)S(1)}, u32[]{:S(2)}, u32[]{:S(2)}) collective-permute-start(f32[2,16,256]{2,1,0:T(8,128)} %get-tuple-element.421), channel_id=1, source_target_pairs={{0,8},{8,16},{16,24},{1,9},{9,17},{17,25},{2,10},{10,18},{18,26},{... | collective-permute-start | bytes 98312 | tf_op jit(solution)/shard_map/ppermute | solution.py:21
  276.1 34.9 %collective-permute-start.63 = (f32[2,16,256]{2,1,0:T(8,128)S(1)}, f32[2,16,256]{2,1,0:T(8,128)S(1)}, u32[]{:S(2)}, u32[]{:S(2)}) collective-permute-start(f32[2,16,256]{2,1,0:T(8,128)S(1)} %get-tuple-element.422), channel_id=1, source_target_pairs={{0,1},{1,2},{2,3},{3,4},{4,5},{5,6},{6,7},{8,9},{9,10},{10,11},{11... | collective-permute-start | bytes 98312 | tf_op jit(solution)/shard_map/ppermute | solution.py:21
  (71 other events, 939.1 us)
